TPU v7x, 32 devices: a whole 2x2x4 slice. The times are simulated.
32 devices in a mesh: section: 2 (over core), mp: 4 (over y, x), dp: 4 (over z).
Axes of the slice: x: 2, y: 2, z: 4, core: 2. Of those that a mesh axis runs over, the one named last changes fastest.
Arguments:
- value_grad: bfloat16 [2, 2048, 3072], P('section', 'dp', 'mp'), may hold values from -6 to 6
- stream: bfloat16 [2, 2048, 3072], P('section', 'dp'), may hold values from -300 to 300
- weights: bfloat16 [2, 3072, 3072], P('section', 'mp'), may hold values from -0.109375 to 0.109375
- gain: float32 [2, 3072], P('section'), may hold values from 0.25 to 1.75
- top_grad: bfloat16 [2048, 3072], P('dp'), may hold values from -6 to 6
- counts: int32 [4], P('dp'), may hold values from 1 to 2, as said below
Outputs:
- weight_grad: bfloat16 [2, 3072, 3072], P('section', ('mp', 'dp'))
- residual_grad: bfloat16 [2, 2048, 3072], P('section', 'dp', 'mp')
Inputs may be any that keep to these rules, and one draw needn't show every extreme that they name: counts[r] counts the live micro-batches of replica r; some replica has all 2.
All inputs are finite; a program needn't handle non-finite values.
Results may differ from a plain program's by a relative error of at most 0.009.
Values may be sent and summed in bfloat16 or wider, within the bound.
A program may use at most 64 MiB of HBM per device.

v0:
```python
import jax
import jax.numpy as jnp
from jax import lax
from jax.sharding import PartitionSpec as P

TOK_MB = 256


def normalize(stream_rows):
    values = stream_rows.astype(jnp.float32)
    average = jnp.mean(values, axis=-1, keepdims=True)
    centred = values - average
    variance = jnp.mean(centred * centred, axis=-1, keepdims=True)
    inv_scale = lax.rsqrt(variance + 1e-06)
    return (centred * inv_scale, inv_scale)


def shards(value_grad, stream, weights, gain, top_grad, counts):
    section_index = lax.axis_index("section")
    model_index = lax.axis_index("mp")
    row_total = stream.shape[1]
    whitened, inv_scale = normalize(stream[0])
    gain_row = gain[0]
    width = whitened.shape[1]
    share = width // lax.axis_size("mp")
    first_col = model_index * share
    cols = lambda a: lax.dynamic_slice_in_dim(a, first_col, share, 1)
    partial = jnp.dot(value_grad[0], weights[0], preferred_element_type=jnp.float32)
    partial = partial.astype(jnp.bfloat16)
    local = partial.astype(jnp.float32) * gain_row
    sums = jnp.stack([jnp.sum(local, -1), jnp.sum(local * whitened, -1)])
    norm_grad = lax.psum_scatter(partial, "mp", scatter_dimension=1, tiled=True)
    sums = lax.psum(sums, "mp") * (1.0 / width)
    normed = (whitened * gain_row).astype(jnp.bfloat16)
    micro_index = jnp.arange(row_total, dtype=jnp.int32) // TOK_MB
    live_mask = (micro_index < counts[0]).astype(jnp.bfloat16)
    masked = value_grad[0] * live_mask[:, None]
    product = lax.dot_general(
        masked, normed, (((0,), (0,)), ((), ())), preferred_element_type=jnp.float32
    )
    weight_grad = lax.psum_scatter(
        product.astype(jnp.bfloat16), "dp", scatter_dimension=0, tiled=True
    )[None]
    scaled = norm_grad.astype(jnp.float32) * cols(gain)
    branch = inv_scale * (scaled - sums[0][:, None] - cols(whitened) * sums[1][:, None])
    above = (cols(top_grad).astype(jnp.float32) + branch).astype(jnp.bfloat16)
    below = lax.ppermute(above, "section", [(1, 0)])
    lower = (below.astype(jnp.float32) + branch).astype(jnp.bfloat16)
    result = jnp.where(section_index == 0, lower, above)
    return (weight_grad, result[None])


def solution(mesh):
    in_specs = (
        P("section", "dp", "mp"),
        P("section", "dp", None),
        P("section", "mp", None),
        P("section", None),
        P("dp", None),
        P("dp"),
    )
    out_specs = (P("section", ("mp", "dp"), None), P("section", "dp", "mp"))
    return jax.shard_map(shards, mesh=mesh, in_specs=in_specs, out_specs=out_specs, check_vma=False)
```

profile of v0, /device:TPU:1, one launch (start us, length us, event | category | flops | bytes accessed | tf_op | source)
XLA Modules:
  0.0 160.6 jit_solution(5336192532830619747)
XLA Ops:
  7.2 0.0 copy-start
  7.2 0.0 copy-start.2
  7.2 0.0 reduce-scatter.5.cloned.1.call-start
  7.2 0.0 copy-start.3
  7.2 2.5 %convert_reduce_fusion = f32[512]{0:T(512)S(1)} fusion(bf16[1,512,3072]{2,1,0:T(8,128)(2,1)} %param.7), kind=kLoop, calls=%fused_computation.2 | loop fusion | flops 3145216 | bytes 3147776 | tf_op jit(solution)/shard_map/reduce_sum | solution.py:11
  9.8 0.2 copy-done
  10.0 1.0 fusion.6
  11.0 0.0 copy-done.2
  11.0 0.0 copy-done.3
  11.0 8.3 %fusion.7 = (f32[512]{0:T(512)S(1)}, f32[512]{0:T(512)S(1)}, f32[512,3072]{1,0:T(8,128)}, bf16[512,3072]{1,0:T(8,128)(2,1)}) fusion(f32[3072]{0:T(1024)S(1)} %bitcast.46, f32[512]{0:T(512)S(1)} %add_rsqrt_fusion, f32[512]{0:T(512)S(1)} %broadcast_multiply_fusion.1, bf16[1,512,3072]{2,1,0:T(8,128)(2,1)S(1)} %copy-done, bf16[1,768,3072]{2,1,0:T(8,128)(2,1)} %param.8, ...), kind=kOutput, calls=%fused_computation.12 | convolution fusion | flops 2430073856 | bytes 18108416 | tf_op jit(solution)/shard_map/dot_general | solution.py:28
  19.3 0.0 reduce-scatter.5.cloned.1.call-update
  19.3 0.0 reduce-scatter.3.cloned.1.call-start
  20.0 6.0 %convolution_convert_fusion = bf16[768,3072]{1,0:T(8,128)(2,1)} fusion(bf16[1,512,3072]{2,1,0:T(8,128)(2,1)S(1)} %copy-done, f32[3072]{0:T(1024)S(1)} %bitcast.47, f32[512]{0:T(512)S(1)} %add_rsqrt_fusion, f32[512]{0:T(512)S(1)} %broadcast_multiply_fusion.1, bf16[1,512,768]{2,1,0:T(8,128)(2,1)} %param.6, bf16[512]{0:T(512)(128)(2,1)S(1)} %fusion.28), kind=kOutput, calls=%fused_computation.13 | convolution fusion | flops 2426535936 | bytes 8668160 | tf_op jit(solution)/shard_map/dot_general | solution.py:38
  26.0 0.0 reduce-scatter.3.cloned.1.call-update
  26.0 9.3 %psum.7 = f32[2,512]{1,0:T(2,128)S(1)} all-reduce(f32[2,512]{1,0:T(2,128)S(1)} %pad_maximum_fusion), channel_id=1, replica_groups=mesh['section'=2,'mp'=4,'dp'=4] {'mp'}, use_global_device_ids=true, to_apply=%region_6.7 | all-reduce | flops 1024 | bytes 8192 | tf_op jit(solution)/shard_map/psum | solution.py:33
  35.4 30.1 %reduce-scatter.5.cloned.1.call-done = bf16[512,768]{1,0:T(8,128)(2,1)} async-done(((bf16[512,3072]{1,0:T(8,128)(2,1)}), bf16[512,768]{1,0:T(8,128)(2,1)}) %reduce-scatter.5.cloned.1.call-update) | async-done | bytes 786448 | tf_op jit(solution)/shard_map/reduce_scatter | solution.py:32
  65.5 0.0 copy-start.1
  65.5 2.4 %add_convert_fusion.1 = bf16[512,768]{1,0:T(8,128)(2,1)S(1)} fusion(bf16[512,3072]{1,0:T(8,128)(2,1)} %param.10, s32[]{:T(128)S(6)} %select_n.24, f32[512]{0:T(512)S(1)} %bitcast.42, f32[512,3072]{1,0:T(8,128)} %get-tuple-element.4, f32[512]{0:T(512)S(1)} %bitcast.40, f32[768]{0:T(1024)S(1)} %dynamic-slice_reduce_fusion, ...), kind=kLoop, calls=%fused_computation.22 | loop fusion | flops 3538944 | bytes 3941380 | tf_op jit(solution)/shard_map/convert_element_type | solution.py:46
  67.9 2.8 %collective-permute-start = (bf16[512,768]{1,0:T(8,128)(2,1)S(1)}, bf16[512,768]{1,0:T(8,128)(2,1)S(1)}, u32[]{:S(2)}, u32[]{:S(2)}) collective-permute-start(bf16[512,768]{1,0:T(8,128)(2,1)S(1)} %add_convert_fusion.1), channel_id=1, source_target_pairs={{16,0},{17,1},{18,2},{19,3},{20,4},{21,5},{22,6},{23,7},{24,8},{25... | collective-permute-start | bytes 2359304 | tf_op jit(solution)/shard_map/ppermute | solution.py:47
  70.7 1.8 %collective-permute-done = bf16[512,768]{1,0:T(8,128)(2,1)S(1)} collective-permute-done((bf16[512,768]{1,0:T(8,128)(2,1)S(1)}, bf16[512,768]{1,0:T(8,128)(2,1)S(1)}, u32[]{:S(2)}, u32[]{:S(2)}) %collective-permute-start) | collective-permute-done | bytes 786464 | tf_op jit(solution)/shard_map/ppermute | solution.py:47
  72.6 0.0 copy-done.1
  72.6 3.2 %fusion.19 = bf16[1,512,768]{2,1,0:T(8,128)(2,1)} fusion(bf16[512,768]{1,0:T(8,128)(2,1)S(1)} %add_convert_fusion.1, bf16[512,768]{1,0:T(8,128)(2,1)S(1)} %collective-permute-done, pred[]{:T(512)S(6)} %eq.3, f32[512]{0:T(512)S(1)} %bitcast.43, f32[512,3072]{1,0:T(8,128)} %get-tuple-element.4, s32[]{:T(128)S(6)} %select_n.24, f32[512]{0:T(512)S(1)} %bitcast.41, ...), kind=kLoop, calls=%fused_computation.25 | loop fusion | flops 3932160 | bytes 4727813 | tf_op jit(solution)/shard_map/broadcast_in_dim | solution.py:50
  75.8 78.0 %reduce-scatter.3.cloned.1.call-done = bf16[192,3072]{1,0:T(8,128)(2,1)} async-done(((bf16[768,3072]{1,0:T(8,128)(2,1)}), bf16[192,3072]{1,0:T(8,128)(2,1)}) %reduce-scatter.3.cloned.1.call-update) | async-done | bytes 1179664 | tf_op jit(solution)/shard_map/reduce_scatter | solution.py:41
  (7 shorter events, 0.1 us)
Async XLA Ops:
  7.2 2.8 %copy-start = (bf16[1,512,3072]{2,1,0:T(8,128)(2,1)S(1)}, bf16[1,512,3072]{2,1,0:T(8,128)(2,1)}, u32[]{:S(2)}) copy-start(bf16[1,512,3072]{2,1,0:T(8,128)(2,1)} %param.7) | copy-start | bytes 9437188
  7.2 3.8 %copy-start.2 = (f32[1,3072]{1,0:T(1,128)S(1)}, f32[1,3072]{1,0:T(1,128)}, u32[]{:S(2)}) copy-start(f32[1,3072]{1,0:T(1,128)} %param.9) | copy-start | bytes 36868
  7.2 58.3 %reduce-scatter.5.cloned.1.call-start = ((), (), s32[]{:S(2)}) async-start(), calls=%async_computation.3 | async-start | bytes 3932160 | tf_op jit(solution)/shard_map/reduce_scatter | solution.py:32
  7.2 3.7 %copy-start.3 = (bf16[1,512,768]{2,1,0:T(8,128)(2,1)S(1)}, bf16[1,512,768]{2,1,0:T(8,128)(2,1)}, u32[]{:S(2)}) copy-start(bf16[1,512,768]{2,1,0:T(8,128)(2,1)} %param.6) | copy-start | bytes 2359300
  19.3 134.5 %reduce-scatter.3.cloned.1.call-start = ((), (), s32[]{:S(2)}) async-start(), calls=%async_computation.2 | async-start | bytes 5898240 | tf_op jit(solution)/shard_map/reduce_scatter | solution.py:41
  65.5 7.1 %copy-start.1 = (bf16[512,768]{1,0:T(8,128)(2,1)S(1)}, bf16[512,768]{1,0:T(8,128)(2,1)}, u32[]{:S(2)}) copy-start(bf16[512,768]{1,0:T(8,128)(2,1)} %reduce-scatter.5.cloned.1.call-done) | copy-start | bytes 2359300
  67.9 4.6 %collective-permute-start = (bf16[512,768]{1,0:T(8,128)(2,1)S(1)}, bf16[512,768]{1,0:T(8,128)(2,1)S(1)}, u32[]{:S(2)}, u32[]{:S(2)}) collective-permute-start(bf16[512,768]{1,0:T(8,128)(2,1)S(1)} %add_convert_fusion.1), channel_id=1, source_target_pairs={{16,0},{17,1},{18,2},{19,3},{20,4},{21,5},{22,6},{23,7},{24,8},{25... | collective-permute-start | bytes 2359304 | tf_op jit(solution)/shard_map/ppermute | solution.py:47
Sparse Core Ops, SparseCore 0:
  19.4 46.0 reduce-scatter.4
  68.4 85.3 reduce-scatter.2
where the time goes:
time: 162 us; the launch traced here: 161 us
  waiting for transfers between devices  110 us (68%)
  between operations  14.8 us (9%)
  matrix products  14.2 us (9%)
  blocking collectives  9.34 us (6%)
  other arithmetic  9.15 us (6%)
  starting transfers between devices  2.87 us (2%)
    reduce_scatter x1, waiting for transfers between devices, shards(): lax.psum_scatter(product.astype(jnp.bfloat16), 'dp', scatter_dimension=0,...  78 us
    reduce_scatter x1, waiting for transfers between devices, shards(): norm_grad = lax.psum_scatter(partial, 'mp', scatter_dimension=1, tiled=True)  30.1 us
    psum x1, blocking collectives, shards(): sums = lax.psum(sums, 'mp') * (1.0 / width)  9.34 us
    dot_general x1, matrix products, shards(): jnp.dot(value_grad[0], weights[0], preferred_element_type=jnp.float32)  8.28 us
    dot_general x1, matrix products, shards(): lax.dot_general(masked, normed, (((0,), (0,)), ((), ())), preferred_eleme...  5.96 us
  transfers between devices with their start and end apart: 3, of which 3 were waited for; matrix products, arithmetic and copies ran while one was open for 7% of the time, Pallas kernels for 0%

commit v1 on v0

v1 whole, which is shorter than its diff:
```python
import functools

import jax
import jax.numpy as jnp
from jax import lax
from jax.experimental import pallas as pl
from jax.experimental.pallas import tpu as pltpu
from jax.sharding import PartitionSpec as P

TOK_MB = 256
LANES = 128
ROWS = 128
LN_ROWS = 64
EPS = 1e-06
F32 = jnp.float32
BF16 = jnp.bfloat16
MESH = pl.DeviceIdType.MESH


def kernel(
    dims,
    vg_hbm,
    st_hbm,
    w_hbm,
    gain_ref,
    top_hbm,
    counts_ref,
    wg_ref,
    res_ref,
    vg_v,
    st_v,
    w_v,
    top_v,
    mean_v,
    inv_v,
    nrm,
    nrm_in,
    vgt,
    vgt_in,
    ssend,
    srecv,
    rt,
    psend,
    precv,
    acc,
    sums,
    sums_in,
    above_in,
    branch_v,
    load_sem,
    n_send,
    n_recv,
    fwd_send,
    vgt_send,
    vgt_recv,
    s_send,
    s_recv,
    rt_send,
    wg_recv,
    p_send,
    p_recv,
    sum_send,
    sum_recv,
    above_send,
    above_recv,
):
    tokens, width, feats, quarter, out_rows = dims
    blocks = width // LANES
    per_quarter = quarter // LANES
    chunks = tokens // ROWS
    sec = lax.axis_index("section")
    m = lax.axis_index("mp")
    z = lax.axis_index("dp")
    inner = lax.rem(z, 3) != 0
    outer = lax.rem(z, 3) == 0
    mate = z + 1 - 2 * lax.rem(z, 2)
    cross = 3 - z
    keep_half = z // 2
    give_half = 1 - z // 2
    own_slot = lax.rem(z, 2)
    mate_slot = 1 - own_slot

    def peer(kk):
        row = lax.rem(m // 2 + kk // 2, 2)
        col = lax.rem(lax.rem(m, 2) + lax.rem(kk, 2), 2)
        return 2 * row + col

    def column(kk, idx):
        return peer(kk) * per_quarter + idx

    def lanes(start, size=LANES):
        return pl.ds(pl.multiple_of(start, LANES), size)

    def row_chunk(i):
        return pl.ds(pl.multiple_of(i * ROWS, ROWS), ROWS)

    def remote(src, dst, send, recv, where):
        return pltpu.make_async_remote_copy(
            src_ref=src,
            dst_ref=dst,
            send_sem=send,
            recv_sem=recv,
            device_id=where,
            device_id_type=MESH,
        )

    load_vg = pltpu.make_async_copy(vg_hbm.at[0], vg_v, load_sem.at[0])
    load_vg.start()
    load_st = pltpu.make_async_copy(st_hbm.at[0], st_v, load_sem.at[1])
    load_st.start()

    def load_w(kk):
        return pltpu.make_async_copy(
            w_hbm.at[0, :, lanes(peer(kk) * quarter, quarter)],
            w_v.at[kk],
            load_sem.at[2 + kk],
        )

    for kk in (3, 2, 1, 0):
        load_w(kk).start()
    load_top = pltpu.make_async_copy(
        top_hbm.at[:, lanes(m * quarter, quarter)], top_v, load_sem.at[6]
    )
    load_top.start()

    barrier = pltpu.get_barrier_semaphore()

    def greet(where):
        pl.semaphore_signal(barrier, inc=1, device_id=where, device_id_type=MESH)

    for kk in (1, 2, 3):
        greet({"mp": peer(kk)})
    greet({"dp": mate})
    greet({"section": 1 - sec})

    @pl.when(inner)
    def _():
        greet({"dp": cross})
        pl.semaphore_wait(barrier, 6)

    @pl.when(outer)
    def _():
        pl.semaphore_wait(barrier, 5)

    load_vg.wait()
    half = feats // 2
    for h in range(2):
        vgt[h] = vg_v[:, h * half : (h + 1) * half].T

    def copy_vgt(h):
        return remote(
            vgt.at[h], vgt_in.at[h], vgt_send.at[h], vgt_recv.at[h], {"dp": mate}
        )

    @pl.when(outer)
    def _():
        copy_vgt(give_half).start()

    load_st.wait()
    live_count = counts_ref[0]

    def norm_chunk(i, carry):
        first = pl.multiple_of(i * LN_ROWS, LN_ROWS)
        rows = pl.ds(first, LN_ROWS)
        total = jnp.zeros((LN_ROWS, LANES), F32)
        for t in range(blocks):
            total = total + st_v[rows, t * LANES : (t + 1) * LANES].astype(F32)
        mean = jnp.sum(total, axis=-1, keepdims=True) * (1.0 / width)
        mean = jnp.broadcast_to(mean, (LN_ROWS, LANES))
        total = jnp.zeros((LN_ROWS, LANES), F32)
        for t in range(blocks):
            centred = st_v[rows, t * LANES : (t + 1) * LANES].astype(F32) - mean
            total = total + centred * centred
        var = jnp.sum(total, axis=-1, keepdims=True) * (1.0 / width)
        inv = jnp.broadcast_to(lax.rsqrt(var + EPS), (LN_ROWS, LANES))
        mean_v[rows] = mean
        inv_v[rows] = inv
        live = (first // TOK_MB < live_count).astype(F32)
        scale = inv * live
        for t in range(blocks):
            cols = slice(t * LANES, (t + 1) * LANES)
            white = (st_v[rows, cols].astype(F32) - mean) * scale
            nrm[t, rows] = (white * gain_ref[:, cols]).astype(BF16)
        return carry

    lax.fori_loop(0, tokens // LN_ROWS, norm_chunk, 0)

    def copy_normed(kk, idx):
        c = column(kk, idx)
        return remote(
            nrm.at[c], nrm_in.at[c], n_send.at[c], n_recv.at[c], {"dp": mate}
        )

    @pl.when(outer)
    def _():
        def send_pair(idx, carry):
            copy_normed(0, idx).start()
            copy_normed(3, idx).start()
            return carry

        lax.fori_loop(0, per_quarter, send_pair, 0)
        copy_vgt(keep_half).start()

    def copy_part(kk, chunk):
        rows = row_chunk(chunk)
        return remote(
            psend.at[kk, rows],
            precv.at[kk, rows],
            p_send.at[kk, chunk],
            p_recv.at[kk, chunk],
            {"mp": peer(kk)},
        )

    acc[...] = jnp.zeros_like(acc)

    def part_step(s, carry):
        kk = 3 - s // chunks
        chunk = lax.rem(s, chunks)
        rows = row_chunk(chunk)
        q = peer(kk)

        @pl.when(chunk == 0)
        def _():
            load_w(kk).wait()

        part = jnp.dot(vg_v[rows], w_v[kk], preferred_element_type=F32).astype(BF16)
        psend[kk, rows] = part
        first = jnp.zeros((ROWS, LANES), F32)
        second = jnp.zeros((ROWS, LANES), F32)
        mean = mean_v[rows]
        inv = inv_v[rows]
        for j in range(per_quarter):
            cols = lanes(q * quarter + j * LANES)
            local = part[:, j * LANES : (j + 1) * LANES].astype(F32) * gain_ref[:, cols]
            white = (st_v[rows, cols].astype(F32) - mean) * inv
            first = first + local
            second = second + local * white
        acc[0, rows] += first
        acc[1, rows] += second

        @pl.when(kk > 0)
        def _():
            copy_part(kk, chunk).start()

        return carry

    lax.fori_loop(0, 4 * chunks, part_step, 0)

    lane = lax.broadcasted_iota(jnp.int32, (tokens, LANES), 1)
    sum0 = jnp.sum(acc[0], axis=-1, keepdims=True)
    sum1 = jnp.sum(acc[1], axis=-1, keepdims=True)
    packed = jnp.where(lane == 0, sum0, jnp.where(lane == 1, sum1, 0.0))
    sums[...] = packed.T[:8]

    def copy_sums(kk):
        return remote(
            sums, sums_in.at[kk], sum_send.at[kk], sum_recv.at[kk], {"mp": peer(kk)}
        )

    for kk in (3, 2, 1):
        copy_sums(kk).start()

    def copy_above(chunk):
        rows = row_chunk(chunk)
        return remote(
            res_ref.at[rows],
            above_in.at[rows],
            above_send.at[chunk],
            above_recv.at[chunk],
            {"section": 1 - sec},
        )

    def residual():
        load_top.wait()
        for kk in (1, 2, 3):
            copy_sums(kk).wait_recv()
        total = (sums[...] + sums_in[1]) + (sums_in[2] + sums_in[3])
        total = jnp.concatenate([total] * (LANES // 8), axis=0) * (1.0 / width)
        total = total.T
        acc[0] = jnp.broadcast_to(total[:, 0:1], (tokens, LANES))
        acc[1] = jnp.broadcast_to(total[:, 1:2], (tokens, LANES))

        def rows_step(chunk, carry):
            rows = row_chunk(chunk)
            for kk in (1, 2, 3):
                copy_part(kk, chunk).wait_recv()
            mean = mean_v[rows]
            inv = inv_v[rows]
            for j in range(per_quarter):
                here = slice(j * LANES, (j + 1) * LANES)
                cols = lanes(m * quarter + j * LANES)
                grad = psend[0, rows, here].astype(F32)
                for kk in (1, 2, 3):
                    grad = grad + precv[kk, rows, here].astype(F32)
                scaled = grad * gain_ref[:, cols]
                white = (st_v[rows, cols].astype(F32) - mean) * inv
                branch = inv * (scaled - acc[0, rows] - white * acc[1, rows])
                branch_v[rows, here] = branch
                res_ref[rows, here] = (top_v[rows, here].astype(F32) + branch).astype(
                    BF16
                )

            @pl.when(sec == 1)
            def _():
                copy_above(chunk).start()

            return carry

        lax.fori_loop(0, chunks, rows_step, 0)

        @pl.when(sec == 0)
        def _():
            def lower(chunk, carry):
                rows = row_chunk(chunk)
                copy_above(chunk).wait_recv()
                res_ref[rows] = (above_in[rows].astype(F32) + branch_v[rows]).astype(
                    BF16
                )
                return carry

            lax.fori_loop(0, chunks, lower, 0)

    def copy_wg(c):
        return remote(
            rt.at[c, mate_slot],
            wg_ref.at[:, lanes(c * LANES)],
            rt_send.at[c],
            wg_recv.at[c],
            {"dp": mate},
        )

    @pl.when(outer)
    def _():
        residual()

        def finish(c, carry):
            copy_wg(c).wait_recv()
            return carry

        lax.fori_loop(0, blocks, finish, 0)
        for h in range(2):
            copy_vgt(h).wait_send()

        def sent(idx, carry):
            copy_normed(0, idx).wait_send()
            copy_normed(3, idx).wait_send()
            return carry

        lax.fori_loop(0, per_quarter, sent, 0)

    @pl.when(inner)
    def _():
        def copy_forward(kk, idx):
            c = column(0, idx)
            return remote(
                nrm_in.at[c],
                nrm_in.at[c],
                fwd_send.at[kk - 1, idx],
                n_recv.at[c],
                {"mp": peer(kk)},
            )

        def copy_cross(c):
            return remote(
                ssend.at[c], srecv.at[c], s_send.at[c], s_recv.at[c], {"dp": cross}
            )

        def wait_normed(c):
            remote(
                nrm.at[c], nrm_in.at[c], n_send.at[c], n_recv.at[c], {"dp": mate}
            ).wait_recv()

        def forward(idx):
            wait_normed(column(0, idx))
            copy_forward(1, idx).start()
            copy_forward(2, idx).start()

        def column_at(i):
            return column(lax.rem(3 * lax.rem(i, 4), 4), i // 4)

        def product(h, c):
            return jnp.dot(vgt[h], nrm[c], preferred_element_type=F32) + jnp.dot(
                vgt_in[h], nrm_in[c], preferred_element_type=F32
            )

        def give(i):
            c = column_at(i)

            @pl.when(lax.rem(i, 4) != 0)
            def _():
                wait_normed(c)

            ssend[c] = product(give_half, c).astype(BF16)
            copy_cross(c).start()

            @pl.when(jnp.logical_and(lax.rem(i, 4) == 3, i < blocks - 4))
            def _():
                forward(i // 4 + 1)

        def keep(i):
            c = column_at(i)
            copy_cross(c).wait_recv()
            total = product(keep_half, c) + srecv[c].astype(F32)
            total = total.astype(BF16)
            rt[c, 0] = total[:out_rows]
            rt[c, 1] = total[out_rows:]
            copy_wg(c).start()
            wg_ref[:, lanes(c * LANES)] = rt[c, own_slot]

        copy_vgt(give_half).wait_recv()
        forward(0)

        def first_round(i, carry):
            give(i)
            return carry

        lax.fori_loop(0, 4, first_round, 0)
        copy_give_wait = copy_vgt(keep_half)
        give(4)
        give(5)
        give(6)
        give(7)
        copy_give_wait.wait_recv()

        def both(i, carry):
            give(i)
            keep(i - 8)
            return carry

        lax.fori_loop(8, blocks, both, 0)
        residual()

        def last(i, carry):
            keep(i)
            return carry

        lax.fori_loop(blocks - 8, blocks, last, 0)

        def sent(c, carry):
            copy_cross(c).wait_send()
            copy_wg(c).wait_send()
            return carry

        lax.fori_loop(0, blocks, sent, 0)

        def forwarded(idx, carry):
            copy_forward(1, idx).wait_send()
            copy_forward(2, idx).wait_send()
            return carry

        lax.fori_loop(0, per_quarter, forwarded, 0)

    for kk in (1, 2, 3):
        copy_sums(kk).wait_send()

        def part_sent(chunk, carry):
            copy_part(kk, chunk).wait_send()
            return carry

        lax.fori_loop(0, chunks, part_sent, 0)

    @pl.when(sec == 1)
    def _():
        def above_sent(chunk, carry):
            copy_above(chunk).wait_send()
            return carry

        lax.fori_loop(0, chunks, above_sent, 0)


def fused(value_grad, stream, weights, gain, top_grad, counts):
    tokens, width = stream.shape[1:]
    feats = value_grad.shape[2]
    quarter = width // lax.axis_size("mp")
    out_rows = feats // lax.axis_size("dp")
    blocks = width // LANES
    per_quarter = quarter // LANES
    chunks = tokens // ROWS
    dma = pltpu.SemaphoreType.DMA
    vmem = pltpu.VMEM
    anywhere = pl.BlockSpec(memory_space=pl.ANY)
    in_vmem = pl.BlockSpec(memory_space=pltpu.VMEM)
    weight_grad, residual_grad = pl.pallas_call(
        functools.partial(kernel, (tokens, width, feats, quarter, out_rows)),
        out_shape=(
            jax.ShapeDtypeStruct((out_rows, width), BF16),
            jax.ShapeDtypeStruct((tokens, quarter), BF16),
        ),
        in_specs=[
            anywhere,
            anywhere,
            anywhere,
            in_vmem,
            anywhere,
            pl.BlockSpec(memory_space=pltpu.SMEM),
        ],
        out_specs=(in_vmem, in_vmem),
        scratch_shapes=[
            vmem((tokens, feats), BF16),
            vmem((tokens, width), BF16),
            vmem((4, feats, quarter), BF16),
            vmem((tokens, quarter), BF16),
            vmem((tokens, LANES), F32),
            vmem((tokens, LANES), F32),
            vmem((blocks, tokens, LANES), BF16),
            vmem((blocks, tokens, LANES), BF16),
            vmem((2, feats // 2, tokens), BF16),
            vmem((2, feats // 2, tokens), BF16),
            vmem((blocks, 2 * out_rows, LANES), BF16),
            vmem((blocks, 2 * out_rows, LANES), BF16),
            vmem((blocks, 2, out_rows, LANES), BF16),
            vmem((4, tokens, quarter), BF16),
            vmem((4, tokens, quarter), BF16),
            vmem((2, tokens, LANES), F32),
            vmem((8, tokens), F32),
            vmem((4, 8, tokens), F32),
            vmem((tokens, quarter), BF16),
            vmem((tokens, quarter), F32),
            dma((7,)),
            dma((blocks,)),
            dma((blocks,)),
            dma((2, per_quarter)),
            dma((2,)),
            dma((2,)),
            dma((blocks,)),
            dma((blocks,)),
            dma((blocks,)),
            dma((blocks,)),
            dma((4, chunks)),
            dma((4, chunks)),
            dma((4,)),
            dma((4,)),
            dma((chunks,)),
            dma((chunks,)),
        ],
        compiler_params=pltpu.CompilerParams(
            collective_id=0, has_side_effects=True, vmem_limit_bytes=52 * 2**20
        ),
    )(value_grad, stream, weights, gain, top_grad, counts)
    return weight_grad[None], residual_grad[None]


def normalize(stream_rows):
    values = stream_rows.astype(F32)
    average = jnp.mean(values, axis=-1, keepdims=True)
    centred = values - average
    variance = jnp.mean(centred * centred, axis=-1, keepdims=True)
    inv_scale = lax.rsqrt(variance + EPS)
    return (centred * inv_scale, inv_scale)


def collectives(value_grad, stream, weights, gain, top_grad, counts):
    section_index = lax.axis_index("section")
    model_index = lax.axis_index("mp")
    row_total = stream.shape[1]
    whitened, inv_scale = normalize(stream[0])
    gain_row = gain[0]
    width = whitened.shape[1]
    share = width // lax.axis_size("mp")
    first_col = model_index * share
    cols = lambda a: lax.dynamic_slice_in_dim(a, first_col, share, 1)
    partial = jnp.dot(value_grad[0], weights[0], preferred_element_type=F32)
    partial = partial.astype(BF16)
    local = partial.astype(F32) * gain_row
    sums = jnp.stack([jnp.sum(local, -1), jnp.sum(local * whitened, -1)])
    norm_grad = lax.psum_scatter(partial, "mp", scatter_dimension=1, tiled=True)
    sums = lax.psum(sums, "mp") * (1.0 / width)
    normed = (whitened * gain_row).astype(BF16)
    micro_index = jnp.arange(row_total, dtype=jnp.int32) // TOK_MB
    live_mask = (micro_index < counts[0]).astype(BF16)
    masked = value_grad[0] * live_mask[:, None]
    product = lax.dot_general(
        masked, normed, (((0,), (0,)), ((), ())), preferred_element_type=F32
    )
    weight_grad = lax.psum_scatter(
        product.astype(BF16), "dp", scatter_dimension=0, tiled=True
    )[None]
    scaled = norm_grad.astype(F32) * cols(gain)
    branch = inv_scale * (scaled - sums[0][:, None] - cols(whitened) * sums[1][:, None])
    above = (cols(top_grad).astype(F32) + branch).astype(BF16)
    below = lax.ppermute(above, "section", [(1, 0)])
    lower = (below.astype(F32) + branch).astype(BF16)
    result = jnp.where(section_index == 0, lower, above)
    return (weight_grad, result[None])


def solution(mesh):
    in_specs = (
        P("section", "dp", "mp"),
        P("section", "dp", None),
        P("section", "mp", None),
        P("section", None),
        P("dp", None),
        P("dp"),
    )
    out_specs = (P("section", ("mp", "dp"), None), P("section", "dp", "mp"))
    grid = (mesh.shape["section"], mesh.shape["mp"], mesh.shape["dp"])
    step = fused if grid == (2, 4, 4) else collectives
    return jax.shard_map(step, mesh=mesh, in_specs=in_specs, out_specs=out_specs, check_vma=False)
```

time: 162 us -> 110 us (0.68)
  waiting for transfers between devices: 110 us -> 0 us
  Pallas kernels: 0 us -> 102 us
  matrix products: 14.2 us -> 0 us
  between operations: 14.8 us -> 1.3 us
  blocking collectives: 9.34 us -> 0 us
  other arithmetic: 9.15 us -> 0 us
  local copies, waits for them, and re-layouts: 0.27 us -> 5.07 us
  starting transfers between devices: 2.87 us -> 0 us
    reduce_scatter x2 -> x0, waiting for transfers between devices: 108 us -> none  [the longest x1 78 us: shards(): lax.psum_scatter(product.astype(jnp.bfloat16), 'dp', scatter_dimension=0,...]
    pallas_call x0 -> x1, Pallas kernels: none -> 102 us  [fused(): pl.pallas_call(functools.partial(kernel, (tokens, width, feats, quarter,...]
    dot_general x2 -> x0, matrix products: 14.2 us -> none  [the longest x1 8.28 us: shards(): jnp.dot(value_grad[0], weights[0], preferred_element_type=jnp.float32)]
    psum x1 -> x0, blocking collectives: 9.34 us -> none  [shards(): sums = lax.psum(sums, 'mp') * (1.0 / width)]
    unnamed x8 -> x6, local copies, waits for them, and re-layouts: 0.24 us -> 5.07 us
    reduce_sum x2 -> x0, other arithmetic: 3.48 us -> none  [the longest x1 2.53 us: normalize(): average = jnp.mean(values, axis=-1, keepdims=True)]
    broadcast_in_dim x1 -> x0, other arithmetic: 3.23 us -> none  [shards(): return (weight_grad, result[None])]
    ppermute x1 -> x0, starting transfers between devices: 2.79 us -> none  [shards(): below = lax.ppermute(above, 'section', [(1, 0)])]
  transfers between devices with their start and end apart: 3 -> 0, of which waited for: 3 -> 0; matrix products, arithmetic and copies ran while one was open for 7% -> 0% of each run, Pallas kernels for 0% -> 0%
where the time goes in v1:
time: 110 us; the launch traced here: 108 us
  Pallas kernels  102 us (93%)
  local copies, waits for them, and re-layouts  5.07 us (5%)
  between operations  1.3 us (1%)
    pallas_call x1, Pallas kernels, fused(): pl.pallas_call(functools.partial(kernel, (tokens, width, feats, quarter,...  102 us
    unnamed x6, local copies, waits for them, and re-layouts  5.07 us

profile of v1, /device:TPU:1, one launch (start us, length us, event | category | flops | bytes accessed | tf_op | source)
XLA Modules:
  0.0 108.0 jit_solution(14089683156602101590)
XLA Ops:
  1.3 0.0 copy-start
  1.3 1.1 %copy-done = bf16[1,512,768]{2,1,0:T(8,128)(2,1)S(1)} copy-done((bf16[1,512,768]{2,1,0:T(8,128)(2,1)S(1)}, bf16[1,512,768]{2,1,0:T(8,128)(2,1)}, u32[]{:S(2)}) %copy-start) | copy-done | bytes 786456
  2.4 0.0 copy-start.1
  2.4 0.7 copy-done.1
  3.1 101.6 %shard_map.77 = (bf16[192,3072]{1,0:T(8,128)(2,1)}, bf16[512,768]{1,0:T(8,128)(2,1)S(1)}) custom-call(bf16[1,512,768]{2,1,0:T(8,128)(2,1)S(1)} %copy-done, bf16[1,512,3072]{2,1,0:T(8,128)(2,1)} %st_hbm.1, bf16[1,768,3072]{2,1,0:T(8,128)(2,1)} %w_hbm.1, f32[1,3072]{1,0:T(1,128)S(1)} %copy-done.1, bf16[512,3072]{1,0:T(8,128)(2,1)} %top_hbm.1, ...), custom_call_target="tpu_custom_call" | custom-call | tf_op jit(solution)/shard_map/pallas_call | solution.py:483
  104.7 2.4 %copy.11 = bf16[1,192,3072]{2,1,0:T(8,128)(2,1)} copy(bf16[1,192,3072]{2,1,0:T(8,128)(2,1)} %bitcast.3) | data formatting | bytes 2359296
  107.1 0.9 copy.12
Async XLA Ops:
  1.3 1.1 %copy-start = (bf16[1,512,768]{2,1,0:T(8,128)(2,1)S(1)}, bf16[1,512,768]{2,1,0:T(8,128)(2,1)}, u32[]{:S(2)}) copy-start(bf16[1,512,768]{2,1,0:T(8,128)(2,1)} %vg_hbm.1) | copy-start | bytes 2359300
  2.4 0.7 copy-start.1

commit v2 on v1

--- a/solution.py
+++ b/solution.py
@@ -22,7 +22,7 @@
     vg_hbm,
     st_hbm,
     w_hbm,
-    gain_ref,
+    gain_hbm,
     top_hbm,
     counts_ref,
     wg_ref,
@@ -31,6 +31,7 @@
     st_v,
     w_v,
     top_v,
+    gain_ref,
     mean_v,
     inv_v,
     nrm,
@@ -108,6 +109,8 @@
     load_vg.start()
     load_st = pltpu.make_async_copy(st_hbm.at[0], st_v, load_sem.at[1])
     load_st.start()
+    load_gain = pltpu.make_async_copy(gain_hbm, gain_ref, load_sem.at[7])
+    load_gain.start()
 
     def load_w(kk):
         return pltpu.make_async_copy(
@@ -152,10 +155,14 @@
             vgt.at[h], vgt_in.at[h], vgt_send.at[h], vgt_recv.at[h], {"dp": mate}
         )
 
-    @pl.when(outer)
+    early = jnp.logical_and(outer, sec == 0)
+    late = jnp.logical_and(outer, sec == 1)
+
+    @pl.when(early)
     def _():
         copy_vgt(give_half).start()
 
+    load_gain.wait()
     load_st.wait()
     live_count = counts_ref[0]
 
@@ -191,25 +198,50 @@
             nrm.at[c], nrm_in.at[c], n_send.at[c], n_recv.at[c], {"dp": mate}
         )
 
-    @pl.when(outer)
-    def _():
+    split = per_quarter - 2
+
+    def send_normed():
         def send_pair(idx, carry):
             copy_normed(0, idx).start()
             copy_normed(3, idx).start()
             return carry
 
-        lax.fori_loop(0, per_quarter, send_pair, 0)
+        lax.fori_loop(0, split, send_pair, 0)
         copy_vgt(keep_half).start()
+        lax.fori_loop(split, per_quarter, send_pair, 0)
+
+    @pl.when(early)
+    def _():
+        send_normed()
+
+    upper = chunks // 2
+    hold = jnp.logical_and(inner, sec == 0)
 
     def copy_part(kk, chunk):
         rows = row_chunk(chunk)
+        first_hop = 1 + chunk // upper
+        hop = jnp.where(kk == 3, first_hop, kk)
         return remote(
             psend.at[kk, rows],
             precv.at[kk, rows],
             p_send.at[kk, chunk],
             p_recv.at[kk, chunk],
-            {"mp": peer(kk)},
-        )
+            {"mp": peer(hop)},
+        )
+
+    def pass_on(chunk):
+        rows = row_chunk(chunk)
+        kk = 2 - chunk // upper
+        copy_part(3, chunk).wait_recv()
+        psend[kk, rows] = (psend[kk, rows].astype(F32) + precv[3, rows].astype(F32)).astype(BF16)
+        copy_part(kk, chunk).start()
+
+    def pass_all():
+        def one(chunk, carry):
+            pass_on(chunk)
+            return carry
+
+        lax.fori_loop(0, chunks, one, 0)
 
     acc[...] = jnp.zeros_like(acc)
 
@@ -238,13 +270,20 @@
         acc[0, rows] += first
         acc[1, rows] += second
 
-        @pl.when(kk > 0)
+        direct = jnp.logical_or(kk == 3, kk == 1 + chunk // upper)
+
+        @pl.when(jnp.logical_and(direct, jnp.logical_or(outer, sec == 1)))
         def _():
             copy_part(kk, chunk).start()
 
         return carry
 
     lax.fori_loop(0, 4 * chunks, part_step, 0)
+
+    @pl.when(late)
+    def _():
+        copy_vgt(give_half).start()
+        send_normed()
 
     lane = lax.broadcasted_iota(jnp.int32, (tokens, LANES), 1)
     sum0 = jnp.sum(acc[0], axis=-1, keepdims=True)
@@ -259,6 +298,10 @@
 
     for kk in (3, 2, 1):
         copy_sums(kk).start()
+
+    @pl.when(jnp.logical_or(outer, sec == 1))
+    def _():
+        pass_all()
 
     def copy_above(chunk):
         rows = row_chunk(chunk)
@@ -282,7 +325,7 @@
 
         def rows_step(chunk, carry):
             rows = row_chunk(chunk)
-            for kk in (1, 2, 3):
+            for kk in (1, 2):
                 copy_part(kk, chunk).wait_recv()
             mean = mean_v[rows]
             inv = inv_v[rows]
@@ -290,7 +333,7 @@
                 here = slice(j * LANES, (j + 1) * LANES)
                 cols = lanes(m * quarter + j * LANES)
                 grad = psend[0, rows, here].astype(F32)
-                for kk in (1, 2, 3):
+                for kk in (1, 2):
                     grad = grad + precv[kk, rows, here].astype(F32)
                 scaled = grad * gain_ref[:, cols]
                 white = (st_v[rows, cols].astype(F32) - mean) * inv
@@ -397,6 +440,25 @@
             def _():
                 forward(i // 4 + 1)
 
+            @pl.when(jnp.logical_and(hold, i == 3))
+            def _():
+                for chunk in range(0, chunks, 2):
+                    copy_part(3, chunk).start()
+
+            @pl.when(jnp.logical_and(hold, i == 7))
+            def _():
+                for chunk in range(1, chunks, 2):
+                    copy_part(3, chunk).start()
+
+            @pl.when(jnp.logical_and(hold, i == 11))
+            def _():
+                for chunk in range(chunks):
+                    copy_part(1 + chunk // upper, chunk).start()
+
+            @pl.when(jnp.logical_and(hold, i == 14))
+            def _():
+                pass_all()
+
         def keep(i):
             c = column_at(i)
             copy_cross(c).wait_recv()
@@ -410,31 +472,29 @@
         copy_vgt(give_half).wait_recv()
         forward(0)
 
-        def first_round(i, carry):
+        head = 4 * split
+
+        def first(i, carry):
             give(i)
             return carry
 
-        lax.fori_loop(0, 4, first_round, 0)
-        copy_give_wait = copy_vgt(keep_half)
-        give(4)
-        give(5)
-        give(6)
-        give(7)
-        copy_give_wait.wait_recv()
+        lax.fori_loop(0, head, first, 0)
+        copy_vgt(keep_half).wait_recv()
 
         def both(i, carry):
             give(i)
-            keep(i - 8)
-            return carry
-
-        lax.fori_loop(8, blocks, both, 0)
+            keep(2 * (i - head))
+            keep(2 * (i - head) + 1)
+            return carry
+
+        lax.fori_loop(head, blocks, both, 0)
         residual()
 
         def last(i, carry):
             keep(i)
             return carry
 
-        lax.fori_loop(blocks - 8, blocks, last, 0)
+        lax.fori_loop(2 * (blocks - head), blocks, last, 0)
 
         def sent(c, carry):
             copy_cross(c).wait_send()
@@ -478,7 +538,7 @@
     chunks = tokens // ROWS
     dma = pltpu.SemaphoreType.DMA
     vmem = pltpu.VMEM
-    anywhere = pl.BlockSpec(memory_space=pl.ANY)
+    in_hbm = pl.BlockSpec(memory_space=pltpu.HBM)
     in_vmem = pl.BlockSpec(memory_space=pltpu.VMEM)
     weight_grad, residual_grad = pl.pallas_call(
         functools.partial(kernel, (tokens, width, feats, quarter, out_rows)),
@@ -487,11 +547,11 @@
             jax.ShapeDtypeStruct((tokens, quarter), BF16),
         ),
         in_specs=[
-            anywhere,
-            anywhere,
-            anywhere,
-            in_vmem,
-            anywhere,
+            in_hbm,
+            in_hbm,
+            in_hbm,
+            in_hbm,
+            in_hbm,
             pl.BlockSpec(memory_space=pltpu.SMEM),
         ],
         out_specs=(in_vmem, in_vmem),
@@ -500,6 +560,7 @@
             vmem((tokens, width), BF16),
             vmem((4, feats, quarter), BF16),
             vmem((tokens, quarter), BF16),
+            vmem((1, width), F32),
             vmem((tokens, LANES), F32),
             vmem((tokens, LANES), F32),
             vmem((blocks, tokens, LANES), BF16),
@@ -516,7 +577,7 @@
             vmem((4, 8, tokens), F32),
             vmem((tokens, quarter), BF16),
             vmem((tokens, quarter), F32),
-            dma((7,)),
+            dma((8,)),
             dma((blocks,)),
             dma((blocks,)),
             dma((2, per_quarter)),
@@ -534,7 +595,7 @@
             dma((chunks,)),
         ],
         compiler_params=pltpu.CompilerParams(
-            collective_id=0, has_side_effects=True, vmem_limit_bytes=52 * 2**20
+            collective_id=0, has_side_effects=True, vmem_limit_bytes=44 * 2**20
         ),
     )(value_grad, stream, weights, gain, top_grad, counts)
     return weight_grad[None], residual_grad[None]

time: 110 us -> 89.8 us (0.82)
  the two profiles are of different devices: /device:TPU:1 before, /device:TPU:0 now
where the time goes in v2:
time: 89.8 us; the launch traced here: 89.5 us
  Pallas kernels  80.7 us (90%)
  local copies, waits for them, and re-layouts  7.51 us (8%)
  between operations  1.3 us (1%)
    pallas_call x1, Pallas kernels, fused(): pl.pallas_call(functools.partial(kernel, (tokens, width, feats, quarter,...  80.7 us
    unnamed x10, local copies, waits for them, and re-layouts  7.51 us

profile of v2, /device:TPU:0, one launch (start us, length us, event | category | flops | bytes accessed | tf_op | source)
XLA Modules:
  0.0 89.5 jit_solution(14197964236270753533)
XLA Ops:
  1.3 0.0 copy-start
  1.3 1.9 %copy-done = bf16[1,512,3072]{2,1,0:T(8,128)(2,1)S(1)} copy-done((bf16[1,512,3072]{2,1,0:T(8,128)(2,1)S(1)}, bf16[1,512,3072]{2,1,0:T(8,128)(2,1)}, u32[]{:S(2)}) %copy-start) | copy-done | bytes 3145752
  3.2 0.0 copy-start.1
  3.2 1.9 %copy-done.1 = bf16[512,3072]{1,0:T(8,128)(2,1)S(1)} copy-done((bf16[512,3072]{1,0:T(8,128)(2,1)S(1)}, bf16[512,3072]{1,0:T(8,128)(2,1)}, u32[]{:S(2)}) %copy-start.1) | copy-done | bytes 3145752
  5.1 0.0 copy-start.2
  5.1 1.1 %copy-done.2 = bf16[1,512,768]{2,1,0:T(8,128)(2,1)S(1)} copy-done((bf16[1,512,768]{2,1,0:T(8,128)(2,1)S(1)}, bf16[1,512,768]{2,1,0:T(8,128)(2,1)}, u32[]{:S(2)}) %copy-start.2) | copy-done | bytes 786456
  6.2 0.0 copy-start.3
  6.2 0.7 copy-done.3
  6.9 80.7 %shard_map.77 = (bf16[192,3072]{1,0:T(8,128)(2,1)S(1)}, bf16[512,768]{1,0:T(8,128)(2,1)S(1)}) custom-call(bf16[1,512,768]{2,1,0:T(8,128)(2,1)S(1)} %copy-done.2, bf16[1,512,3072]{2,1,0:T(8,128)(2,1)S(1)} %copy-done, bf16[1,768,3072]{2,1,0:T(8,128)(2,1)} %w_hbm.1, f32[1,3072]{1,0:T(1,128)S(1)} %copy-done.3, bf16[512,3072]{1,0:T(8,128)(2,1)S(1)} %copy-done.1, ...), custom_call_target="tpu_custom_call" | custom-call | tf_op jit(solution)/shard_map/pallas_call | solution.py:543
  87.6 1.0 %copy.11 = bf16[1,192,3072]{2,1,0:T(8,128)(2,1)} copy(bf16[1,192,3072]{2,1,0:T(8,128)(2,1)S(1)} %bitcast.2) | data formatting | bytes 2359296
  88.6 0.9 copy.12
Async XLA Ops:
  1.3 1.9 %copy-start = (bf16[1,512,3072]{2,1,0:T(8,128)(2,1)S(1)}, bf16[1,512,3072]{2,1,0:T(8,128)(2,1)}, u32[]{:S(2)}) copy-start(bf16[1,512,3072]{2,1,0:T(8,128)(2,1)} %st_hbm.1) | copy-start | bytes 9437188
  3.2 1.9 %copy-start.1 = (bf16[512,3072]{1,0:T(8,128)(2,1)S(1)}, bf16[512,3072]{1,0:T(8,128)(2,1)}, u32[]{:S(2)}) copy-start(bf16[512,3072]{1,0:T(8,128)(2,1)} %top_hbm.1) | copy-start | bytes 9437188
  5.1 1.1 %copy-start.2 = (bf16[1,512,768]{2,1,0:T(8,128)(2,1)S(1)}, bf16[1,512,768]{2,1,0:T(8,128)(2,1)}, u32[]{:S(2)}) copy-start(bf16[1,512,768]{2,1,0:T(8,128)(2,1)} %vg_hbm.1) | copy-start | bytes 2359300
  6.2 0.7 copy-start.3

commit v3 on v2

--- a/solution.py
+++ b/solution.py
@@ -148,11 +148,24 @@
     load_vg.wait()
     half = feats // 2
     for h in range(2):
-        vgt[h] = vg_v[:, h * half : (h + 1) * half].T
-
-    def copy_vgt(h):
+        vgt[h] = vg_v[:, h * half : (h + 1) * half].T.reshape(2, out_rows, tokens)
+
+    def copy_give():
         return remote(
-            vgt.at[h], vgt_in.at[h], vgt_send.at[h], vgt_recv.at[h], {"dp": mate}
+            vgt.at[give_half],
+            vgt_in.at[give_half],
+            vgt_send.at[0],
+            vgt_recv.at[0],
+            {"dp": mate},
+        )
+
+    def copy_keep(slot):
+        return remote(
+            vgt.at[keep_half, slot],
+            vgt_in.at[keep_half, slot],
+            vgt_send.at[1],
+            vgt_recv.at[1],
+            {"dp": mate},
         )
 
     early = jnp.logical_and(outer, sec == 0)
@@ -160,7 +173,7 @@
 
     @pl.when(early)
     def _():
-        copy_vgt(give_half).start()
+        copy_give().start()
 
     load_gain.wait()
     load_st.wait()
@@ -207,7 +220,7 @@
             return carry
 
         lax.fori_loop(0, split, send_pair, 0)
-        copy_vgt(keep_half).start()
+        copy_keep(mate_slot).start()
         lax.fori_loop(split, per_quarter, send_pair, 0)
 
     @pl.when(early)
@@ -282,7 +295,7 @@
 
     @pl.when(late)
     def _():
-        copy_vgt(give_half).start()
+        copy_give().start()
         send_normed()
 
     lane = lax.broadcasted_iota(jnp.int32, (tokens, LANES), 1)
@@ -351,6 +364,7 @@
 
         lax.fori_loop(0, chunks, rows_step, 0)
 
+    def residual_lower():
         @pl.when(sec == 0)
         def _():
             def lower(chunk, carry):
@@ -365,24 +379,31 @@
 
     def copy_wg(c):
         return remote(
-            rt.at[c, mate_slot],
-            wg_ref.at[:, lanes(c * LANES)],
+            rt.at[0, c],
+            rt.at[1, c],
             rt_send.at[c],
             wg_recv.at[c],
             {"dp": mate},
         )
 
+    def column_at(i):
+        return column(lax.rem(3 * lax.rem(i, 4), 4), i // 4)
+
     @pl.when(outer)
     def _():
         residual()
-
-        def finish(c, carry):
+        residual_lower()
+
+        def finish(i, carry):
+            c = column_at(i)
+            own = jnp.dot(vgt[keep_half, own_slot], nrm[c], preferred_element_type=F32)
             copy_wg(c).wait_recv()
+            wg_ref[:, lanes(c * LANES)] = (own + rt[1, c].astype(F32)).astype(BF16)
             return carry
 
         lax.fori_loop(0, blocks, finish, 0)
-        for h in range(2):
-            copy_vgt(h).wait_send()
+        copy_give().wait_send()
+        copy_keep(mate_slot).wait_send()
 
         def sent(idx, carry):
             copy_normed(0, idx).wait_send()
@@ -418,13 +439,8 @@
             copy_forward(1, idx).start()
             copy_forward(2, idx).start()
 
-        def column_at(i):
-            return column(lax.rem(3 * lax.rem(i, 4), 4), i // 4)
-
-        def product(h, c):
-            return jnp.dot(vgt[h], nrm[c], preferred_element_type=F32) + jnp.dot(
-                vgt_in[h], nrm_in[c], preferred_element_type=F32
-            )
+        def dot(features, rows):
+            return jnp.dot(features, rows, preferred_element_type=F32)
 
         def give(i):
             c = column_at(i)
@@ -433,24 +449,31 @@
             def _():
                 wait_normed(c)
 
-            ssend[c] = product(give_half, c).astype(BF16)
+            rows = (2 * out_rows, tokens)
+            total = dot(vgt[give_half].reshape(rows), nrm[c])
+            total = total + dot(vgt_in[give_half].reshape(rows), nrm_in[c])
+            ssend[c] = total.astype(BF16).reshape(2, out_rows, LANES)
             copy_cross(c).start()
 
-            @pl.when(jnp.logical_and(lax.rem(i, 4) == 3, i < blocks - 4))
+            following = i // 4 + 1
+            soon = jnp.logical_and(sec == 0, following < split)
+            turn = lax.rem(i, 4) == jnp.where(soon, 1, 3)
+
+            @pl.when(jnp.logical_and(turn, following < per_quarter))
             def _():
-                forward(i // 4 + 1)
-
-            @pl.when(jnp.logical_and(hold, i == 3))
+                forward(following)
+
+            @pl.when(jnp.logical_and(hold, i == 5))
             def _():
                 for chunk in range(0, chunks, 2):
                     copy_part(3, chunk).start()
 
-            @pl.when(jnp.logical_and(hold, i == 7))
+            @pl.when(jnp.logical_and(hold, i == 9))
             def _():
                 for chunk in range(1, chunks, 2):
                     copy_part(3, chunk).start()
 
-            @pl.when(jnp.logical_and(hold, i == 11))
+            @pl.when(jnp.logical_and(hold, i == 12))
             def _():
                 for chunk in range(chunks):
                     copy_part(1 + chunk // upper, chunk).start()
@@ -462,14 +485,15 @@
         def keep(i):
             c = column_at(i)
             copy_cross(c).wait_recv()
-            total = product(keep_half, c) + srecv[c].astype(F32)
-            total = total.astype(BF16)
-            rt[c, 0] = total[:out_rows]
-            rt[c, 1] = total[out_rows:]
+            theirs = dot(vgt[keep_half, mate_slot], nrm[c])
+            rt[0, c] = (theirs + srecv[c, mate_slot].astype(F32)).astype(BF16)
             copy_wg(c).start()
-            wg_ref[:, lanes(c * LANES)] = rt[c, own_slot]
-
-        copy_vgt(give_half).wait_recv()
+            mine = dot(vgt[keep_half, own_slot], nrm[c])
+            mine = mine + dot(vgt_in[keep_half, own_slot], nrm_in[c])
+            mine = mine + srecv[c, own_slot].astype(F32)
+            wg_ref[:, lanes(c * LANES)] = mine.astype(BF16)
+
+        copy_give().wait_recv()
         forward(0)
 
         head = 4 * split
@@ -479,22 +503,30 @@
             return carry
 
         lax.fori_loop(0, head, first, 0)
-        copy_vgt(keep_half).wait_recv()
+
+        @pl.when(sec == 1)
+        def _():
+            residual()
+
+        copy_keep(own_slot).wait_recv()
 
         def both(i, carry):
             give(i)
-            keep(2 * (i - head))
-            keep(2 * (i - head) + 1)
+            keep(i - head)
             return carry
 
         lax.fori_loop(head, blocks, both, 0)
-        residual()
+
+        @pl.when(sec == 0)
+        def _():
+            residual()
 
         def last(i, carry):
             keep(i)
             return carry
 
-        lax.fori_loop(2 * (blocks - head), blocks, last, 0)
+        lax.fori_loop(blocks - head, blocks, last, 0)
+        residual_lower()
 
         def sent(c, carry):
             copy_cross(c).wait_send()
@@ -565,11 +597,11 @@
             vmem((tokens, LANES), F32),
             vmem((blocks, tokens, LANES), BF16),
             vmem((blocks, tokens, LANES), BF16),
-            vmem((2, feats // 2, tokens), BF16),
-            vmem((2, feats // 2, tokens), BF16),
-            vmem((blocks, 2 * out_rows, LANES), BF16),
-            vmem((blocks, 2 * out_rows, LANES), BF16),
+            vmem((2, 2, out_rows, tokens), BF16),
+            vmem((2, 2, out_rows, tokens), BF16),
             vmem((blocks, 2, out_rows, LANES), BF16),
+            vmem((blocks, 2, out_rows, LANES), BF16),
+            vmem((2, blocks, out_rows, LANES), BF16),
             vmem((4, tokens, quarter), BF16),
             vmem((4, tokens, quarter), BF16),
             vmem((2, tokens, LANES), F32),
@@ -595,7 +627,7 @@
             dma((chunks,)),
         ],
         compiler_params=pltpu.CompilerParams(
-            collective_id=0, has_side_effects=True, vmem_limit_bytes=44 * 2**20
+            collective_id=0, has_side_effects=True, vmem_limit_bytes=51 * 2**20
         ),
     )(value_grad, stream, weights, gain, top_grad, counts)
     return weight_grad[None], residual_grad[None]

time: 89.8 us -> 85.2 us (0.949)
  the two profiles are of different devices: /device:TPU:0 before, /device:TPU:1 now
where the time goes in v3:
time: 85.2 us; the launch traced here: 85 us
  Pallas kernels  79.9 us (94%)
  local copies, waits for them, and re-layouts  3.73 us (4%)
  between operations  1.3 us (2%)
    pallas_call x1, Pallas kernels, fused(): pl.pallas_call(functools.partial(kernel, (tokens, width, feats, quarter,...  79.9 us
    unnamed x6, local copies, waits for them, and re-layouts  3.73 us

profile of v3, /device:TPU:1, one launch (start us, length us, event | category | flops | bytes accessed | tf_op | source)
XLA Modules:
  0.0 85.0 jit_solution(12807822684324574271)
XLA Ops:
  1.3 0.0 copy-start
  1.3 1.1 %copy-done = bf16[1,512,768]{2,1,0:T(8,128)(2,1)S(1)} copy-done((bf16[1,512,768]{2,1,0:T(8,128)(2,1)S(1)}, bf16[1,512,768]{2,1,0:T(8,128)(2,1)}, u32[]{:S(2)}) %copy-start) | copy-done | bytes 786456
  2.4 0.0 copy-start.1
  2.4 0.7 copy-done.1
  3.1 79.9 %shard_map.77 = (bf16[192,3072]{1,0:T(8,128)(2,1)S(1)}, bf16[512,768]{1,0:T(8,128)(2,1)S(1)}) custom-call(bf16[1,512,768]{2,1,0:T(8,128)(2,1)S(1)} %copy-done, bf16[1,512,3072]{2,1,0:T(8,128)(2,1)} %st_hbm.1, bf16[1,768,3072]{2,1,0:T(8,128)(2,1)} %w_hbm.1, f32[1,3072]{1,0:T(1,128)S(1)} %copy-done.1, bf16[512,3072]{1,0:T(8,128)(2,1)} %top_hbm.1, ...), custom_call_target="tpu_custom_call" | custom-call | tf_op jit(solution)/shard_map/pallas_call | solution.py:575
  83.1 1.0 %copy.11 = bf16[1,192,3072]{2,1,0:T(8,128)(2,1)} copy(bf16[1,192,3072]{2,1,0:T(8,128)(2,1)S(1)} %bitcast.2) | data formatting | bytes 2359296
  84.1 0.9 %copy.12 = bf16[1,512,768]{2,1,0:T(8,128)(2,1)} copy(bf16[1,512,768]{2,1,0:T(8,128)(2,1)S(1)} %bitcast.3) | data formatting | bytes 1572864
Async XLA Ops:
  1.3 1.1 %copy-start = (bf16[1,512,768]{2,1,0:T(8,128)(2,1)S(1)}, bf16[1,512,768]{2,1,0:T(8,128)(2,1)}, u32[]{:S(2)}) copy-start(bf16[1,512,768]{2,1,0:T(8,128)(2,1)} %vg_hbm.1) | copy-start | bytes 2359300
  2.4 0.7 copy-start.1

commit v4 on v3

--- a/solution.py
+++ b/solution.py
@@ -211,23 +211,20 @@
             nrm.at[c], nrm_in.at[c], n_send.at[c], n_recv.at[c], {"dp": mate}
         )
 
-    split = per_quarter - 2
-
-    def send_normed():
+    def send_normed(first, last):
         def send_pair(idx, carry):
             copy_normed(0, idx).start()
             copy_normed(3, idx).start()
             return carry
 
-        lax.fori_loop(0, split, send_pair, 0)
-        copy_keep(mate_slot).start()
-        lax.fori_loop(split, per_quarter, send_pair, 0)
+        lax.fori_loop(first, last, send_pair, 0)
 
     @pl.when(early)
     def _():
-        send_normed()
+        send_normed(0, 3)
 
     upper = chunks // 2
+    lag = 6
     hold = jnp.logical_and(inner, sec == 0)
 
     def copy_part(kk, chunk):
@@ -255,6 +252,74 @@
             return carry
 
         lax.fori_loop(0, chunks, one, 0)
+
+    def column_at(i):
+        return column(lax.rem(3 * lax.rem(i, 4), 4), i // 4)
+
+    def copy_wg(c):
+        return remote(
+            rt.at[0, c],
+            rt.at[1, c],
+            rt_send.at[c],
+            wg_recv.at[c],
+            {"dp": mate},
+        )
+
+    def copy_forward(kk, idx):
+        c = column(0, idx)
+        return remote(
+            nrm_in.at[c],
+            nrm_in.at[c],
+            fwd_send.at[kk - 1, idx],
+            n_recv.at[c],
+            {"mp": peer(kk)},
+        )
+
+    def copy_cross(c):
+        return remote(
+            ssend.at[c], srecv.at[c], s_send.at[c], s_recv.at[c], {"dp": cross}
+        )
+
+    def wait_normed(c):
+        remote(
+            nrm.at[c], nrm_in.at[c], n_send.at[c], n_recv.at[c], {"dp": mate}
+        ).wait_recv()
+
+    def forward(idx):
+        wait_normed(column(0, idx))
+        copy_forward(1, idx).start()
+        copy_forward(2, idx).start()
+
+    def dot(features, rows):
+        return jnp.dot(features, rows, preferred_element_type=F32)
+
+    def give(i):
+        c = column_at(i)
+
+        @pl.when(lax.rem(i, 4) != 0)
+        def _():
+            wait_normed(c)
+
+        rows = (2 * out_rows, tokens)
+        total = dot(vgt[give_half].reshape(rows), nrm[c])
+        total = total + dot(vgt_in[give_half].reshape(rows), nrm_in[c])
+        ssend[c] = total.astype(BF16).reshape(2, out_rows, LANES)
+        copy_cross(c).start()
+
+
+    def theirs(i):
+        c = column_at(i)
+        copy_cross(c).wait_recv()
+        total = dot(vgt[keep_half, mate_slot], nrm[c])
+        rt[0, c] = (total + srecv[c, mate_slot].astype(F32)).astype(BF16)
+        copy_wg(c).start()
+
+    def mine(i):
+        c = column_at(i)
+        total = dot(vgt[keep_half, own_slot], nrm[c])
+        total = total + dot(vgt_in[keep_half, own_slot], nrm_in[c])
+        total = total + srecv[c, own_slot].astype(F32)
+        wg_ref[:, lanes(c * LANES)] = total.astype(BF16)
 
     acc[...] = jnp.zeros_like(acc)
 
@@ -285,36 +350,58 @@
 
         direct = jnp.logical_or(kk == 3, kk == 1 + chunk // upper)
 
-        @pl.when(jnp.logical_and(direct, jnp.logical_or(outer, sec == 1)))
+        ready = jnp.logical_or(outer, jnp.logical_and(sec == 1, kk == 3))
+
+        @pl.when(jnp.logical_and(direct, ready))
         def _():
             copy_part(kk, chunk).start()
 
         return carry
 
-    lax.fori_loop(0, 4 * chunks, part_step, 0)
+    lax.fori_loop(0, 2 * chunks, part_step, 0)
+
+    @pl.when(hold)
+    def _():
+        copy_give().wait_recv()
+        forward(0)
+        give(0)
+
+    def copy_sums(kk):
+        return remote(
+            sums, sums_in.at[kk], sum_send.at[kk], sum_recv.at[kk], {"mp": peer(kk)}
+        )
+
+    def send_sums():
+        lane = lax.broadcasted_iota(jnp.int32, (tokens, LANES), 1)
+        sum0 = jnp.sum(acc[0], axis=-1, keepdims=True)
+        sum1 = jnp.sum(acc[1], axis=-1, keepdims=True)
+        packed = jnp.where(lane == 0, sum0, jnp.where(lane == 1, sum1, 0.0))
+        sums[...] = packed.T[:8]
+        for kk in (3, 2, 1):
+            copy_sums(kk).start()
+
+    @pl.when(jnp.logical_or(outer, sec == 1))
+    def _():
+        lax.fori_loop(2 * chunks, 4 * chunks, part_step, 0)
 
     @pl.when(late)
     def _():
         copy_give().start()
-        send_normed()
-
-    lane = lax.broadcasted_iota(jnp.int32, (tokens, LANES), 1)
-    sum0 = jnp.sum(acc[0], axis=-1, keepdims=True)
-    sum1 = jnp.sum(acc[1], axis=-1, keepdims=True)
-    packed = jnp.where(lane == 0, sum0, jnp.where(lane == 1, sum1, 0.0))
-    sums[...] = packed.T[:8]
-
-    def copy_sums(kk):
-        return remote(
-            sums, sums_in.at[kk], sum_send.at[kk], sum_recv.at[kk], {"mp": peer(kk)}
-        )
-
-    for kk in (3, 2, 1):
-        copy_sums(kk).start()
+        send_normed(0, per_quarter)
+        copy_keep(mate_slot).start()
 
     @pl.when(jnp.logical_or(outer, sec == 1))
     def _():
+        send_sums()
+
+    @pl.when(outer)
+    def _():
         pass_all()
+
+    @pl.when(early)
+    def _():
+        send_normed(3, per_quarter)
+        copy_keep(mate_slot).start()
 
     def copy_above(chunk):
         rows = row_chunk(chunk)
@@ -377,18 +464,6 @@
 
             lax.fori_loop(0, chunks, lower, 0)
 
-    def copy_wg(c):
-        return remote(
-            rt.at[0, c],
-            rt.at[1, c],
-            rt_send.at[c],
-            wg_recv.at[c],
-            {"dp": mate},
-        )
-
-    def column_at(i):
-        return column(lax.rem(3 * lax.rem(i, 4), 4), i // 4)
-
     @pl.when(outer)
     def _():
         residual()
@@ -414,49 +489,10 @@
 
     @pl.when(inner)
     def _():
-        def copy_forward(kk, idx):
-            c = column(0, idx)
-            return remote(
-                nrm_in.at[c],
-                nrm_in.at[c],
-                fwd_send.at[kk - 1, idx],
-                n_recv.at[c],
-                {"mp": peer(kk)},
-            )
-
-        def copy_cross(c):
-            return remote(
-                ssend.at[c], srecv.at[c], s_send.at[c], s_recv.at[c], {"dp": cross}
-            )
-
-        def wait_normed(c):
-            remote(
-                nrm.at[c], nrm_in.at[c], n_send.at[c], n_recv.at[c], {"dp": mate}
-            ).wait_recv()
-
-        def forward(idx):
-            wait_normed(column(0, idx))
-            copy_forward(1, idx).start()
-            copy_forward(2, idx).start()
-
-        def dot(features, rows):
-            return jnp.dot(features, rows, preferred_element_type=F32)
-
-        def give(i):
-            c = column_at(i)
-
-            @pl.when(lax.rem(i, 4) != 0)
-            def _():
-                wait_normed(c)
-
-            rows = (2 * out_rows, tokens)
-            total = dot(vgt[give_half].reshape(rows), nrm[c])
-            total = total + dot(vgt_in[give_half].reshape(rows), nrm_in[c])
-            ssend[c] = total.astype(BF16).reshape(2, out_rows, LANES)
-            copy_cross(c).start()
-
+        def step(i):
+            give(i)
             following = i // 4 + 1
-            soon = jnp.logical_and(sec == 0, following < split)
+            soon = jnp.logical_and(sec == 0, following == 1)
             turn = lax.rem(i, 4) == jnp.where(soon, 1, 3)
 
             @pl.when(jnp.logical_and(turn, following < per_quarter))
@@ -473,59 +509,90 @@
                 for chunk in range(1, chunks, 2):
                     copy_part(3, chunk).start()
 
-            @pl.when(jnp.logical_and(hold, i == 12))
-            def _():
-                for chunk in range(chunks):
+            @pl.when(jnp.logical_and(hold, jnp.logical_and(i >= 6, i < 6 + 2 * chunks)))
+            def _():
+                part_step(i - 6 + 2 * chunks, 0)
+
+            @pl.when(jnp.logical_and(hold, i == 14))
+            def _():
+                send_sums()
+
+            @pl.when(jnp.logical_and(hold, i == 15))
+            def _():
+                for chunk in range(0, chunks, 2):
                     copy_part(1 + chunk // upper, chunk).start()
 
-            @pl.when(jnp.logical_and(hold, i == 14))
+            @pl.when(jnp.logical_and(hold, i == 19))
+            def _():
+                for chunk in range(1, chunks, 2):
+                    copy_part(1 + chunk // upper, chunk).start()
+
+            @pl.when(jnp.logical_and(hold, i == 20))
             def _():
                 pass_all()
 
-        def keep(i):
-            c = column_at(i)
-            copy_cross(c).wait_recv()
-            theirs = dot(vgt[keep_half, mate_slot], nrm[c])
-            rt[0, c] = (theirs + srecv[c, mate_slot].astype(F32)).astype(BF16)
-            copy_wg(c).start()
-            mine = dot(vgt[keep_half, own_slot], nrm[c])
-            mine = mine + dot(vgt_in[keep_half, own_slot], nrm_in[c])
-            mine = mine + srecv[c, own_slot].astype(F32)
-            wg_ref[:, lanes(c * LANES)] = mine.astype(BF16)
-
-        copy_give().wait_recv()
-        forward(0)
-
-        head = 4 * split
-
-        def first(i, carry):
-            give(i)
-            return carry
-
-        lax.fori_loop(0, head, first, 0)
+            @pl.when(i >= lag)
+            def _():
+                theirs(i - lag)
+
+            @pl.when(jnp.logical_and(sec == 1, i == 3))
+            def _():
+                for chunk in range(0, chunks, 2):
+                    copy_part(1 + chunk // upper, chunk).start()
+
+            @pl.when(jnp.logical_and(sec == 1, i == 7))
+            def _():
+                for chunk in range(1, chunks, 2):
+                    copy_part(1 + chunk // upper, chunk).start()
+
+            @pl.when(jnp.logical_and(sec == 1, i == 11))
+            def _():
+                for chunk in range(0, chunks, 2):
+                    pass_on(chunk)
+
+            @pl.when(jnp.logical_and(sec == 1, i == 14))
+            def _():
+                for chunk in range(1, chunks, 2):
+                    pass_on(chunk)
+
+            @pl.when(jnp.logical_and(sec == 1, i == 20))
+            def _():
+                residual()
+
+            first_mine = jnp.where(sec == 0, blocks - 4, blocks - 9)
+
+            @pl.when(i == first_mine)
+            def _():
+                copy_keep(own_slot).wait_recv()
+
+            @pl.when(jnp.logical_and(i >= first_mine, i < first_mine + 3))
+            def _():
+                for k in range(4):
+                    mine(4 * (i - first_mine) + k)
 
         @pl.when(sec == 1)
         def _():
-            residual()
-
-        copy_keep(own_slot).wait_recv()
-
-        def both(i, carry):
-            give(i)
-            keep(i - head)
-            return carry
-
-        lax.fori_loop(head, blocks, both, 0)
+            copy_give().wait_recv()
+            forward(0)
+
+        def main(i, carry):
+            step(i)
+            return carry
+
+        lax.fori_loop(1 - sec, blocks, main, 0)
+
+        def last_blocks(i, carry):
+            theirs(i)
+            for k in range(2):
+                mine(2 * i - blocks + k)
+            return carry
+
+        lax.fori_loop(blocks - lag, blocks, last_blocks, 0)
 
         @pl.when(sec == 0)
         def _():
             residual()
 
-        def last(i, carry):
-            keep(i)
-            return carry
-
-        lax.fori_loop(blocks - head, blocks, last, 0)
         residual_lower()
 
         def sent(c, carry):
@@ -572,6 +639,10 @@
     vmem = pltpu.VMEM
     in_hbm = pl.BlockSpec(memory_space=pltpu.HBM)
     in_vmem = pl.BlockSpec(memory_space=pltpu.VMEM)
+    placed = [
+        pltpu.with_memory_space_constraint(a, pltpu.HBM)
+        for a in (value_grad, stream, weights, gain, top_grad)
+    ]
     weight_grad, residual_grad = pl.pallas_call(
         functools.partial(kernel, (tokens, width, feats, quarter, out_rows)),
         out_shape=(
@@ -629,7 +700,7 @@
         compiler_params=pltpu.CompilerParams(
             collective_id=0, has_side_effects=True, vmem_limit_bytes=51 * 2**20
         ),
-    )(value_grad, stream, weights, gain, top_grad, counts)
+    )(*placed, counts)
     return weight_grad[None], residual_grad[None]
 
 

time: 85.2 us -> 77.7 us (0.912)
  Pallas kernels: 79.9 us -> 74.4 us
  local copies, waits for them, and re-layouts: 3.73 us -> 1.89 us
    pallas_call x1, Pallas kernels: 79.9 us -> 74.4 us  [fused(): pl.pallas_call(functools.partial(kernel, (tokens, width, feats, quarter,...]
    unnamed x6 -> x2, local copies, waits for them, and re-layouts: 3.73 us -> 1.89 us
where the time goes in v4:
time: 77.7 us; the launch traced here: 77.6 us
  Pallas kernels  74.4 us (96%)
  local copies, waits for them, and re-layouts  1.89 us (2%)
  between operations  1.29 us (2%)
    pallas_call x1, Pallas kernels, fused(): pl.pallas_call(functools.partial(kernel, (tokens, width, feats, quarter,...  74.4 us
    unnamed x2, local copies, waits for them, and re-layouts  1.89 us

profile of v4, /device:TPU:1, one launch (start us, length us, event | category | flops | bytes accessed | tf_op | source)
XLA Modules:
  0.0 77.6 jit_solution(84446961588156559)
XLA Ops:
  1.3 74.4 %shard_map.77 = (bf16[192,3072]{1,0:T(8,128)(2,1)S(1)}, bf16[512,768]{1,0:T(8,128)(2,1)S(1)}) custom-call(bf16[1,512,768]{2,1,0:T(8,128)(2,1)} %vg_hbm.1, bf16[1,512,3072]{2,1,0:T(8,128)(2,1)} %st_hbm.1, bf16[1,768,3072]{2,1,0:T(8,128)(2,1)} %w_hbm.1, f32[1,3072]{1,0:T(1,128)} %gain_hbm.1, bf16[512,3072]{1,0:T(8,128)(2,1)} %top_hbm.1, s32[1]{0:T(128)S(6)} %copy.10.counts_ref), custom_call_target="tpu_custom_call" | custom-call | tf_op jit(solution)/shard_map/pallas_call | solution.py:646
  75.7 1.0 %copy.11 = bf16[1,192,3072]{2,1,0:T(8,128)(2,1)} copy(bf16[1,192,3072]{2,1,0:T(8,128)(2,1)S(1)} %bitcast.2) | data formatting | bytes 2359296
  76.7 0.9 %copy.12 = bf16[1,512,768]{2,1,0:T(8,128)(2,1)} copy(bf16[1,512,768]{2,1,0:T(8,128)(2,1)S(1)} %bitcast.3) | data formatting | bytes 1572864

commit v5 on v4

--- a/solution.py
+++ b/solution.py
@@ -105,6 +105,9 @@
             device_id_type=MESH,
         )
 
+    def sent(src, dst, sem):
+        remote(src, dst, sem, vgt_recv.at[0], {"dp": mate}).wait_send()
+
     load_vg = pltpu.make_async_copy(vg_hbm.at[0], vg_v, load_sem.at[0])
     load_vg.start()
     load_st = pltpu.make_async_copy(st_hbm.at[0], st_v, load_sem.at[1])
@@ -208,7 +211,7 @@
     def copy_normed(kk, idx):
         c = column(kk, idx)
         return remote(
-            nrm.at[c], nrm_in.at[c], n_send.at[c], n_recv.at[c], {"dp": mate}
+            nrm.at[c], nrm_in.at[c], n_send, n_recv.at[c], {"dp": mate}
         )
 
     def send_normed(first, last):
@@ -224,7 +227,7 @@
         send_normed(0, 3)
 
     upper = chunks // 2
-    lag = 6
+    lag = 10
     hold = jnp.logical_and(inner, sec == 0)
 
     def copy_part(kk, chunk):
@@ -234,8 +237,8 @@
         return remote(
             psend.at[kk, rows],
             precv.at[kk, rows],
-            p_send.at[kk, chunk],
-            p_recv.at[kk, chunk],
+            p_send,
+            p_recv.at[kk - 1, chunk],
             {"mp": peer(hop)},
         )
 
@@ -253,14 +256,23 @@
 
         lax.fori_loop(0, chunks, one, 0)
 
+    def source(i):
+        opening = (1 - sec) * (1 - jnp.minimum(i // 8, 1))
+        late_half = lax.rem(i, 8) // 4
+        odd = lax.rem(i, 2)
+        kk = opening * ((1 - late_half) * 3 * odd + late_half * (2 - odd))
+        kk = kk + (1 - opening) * lax.rem(3 * lax.rem(i, 4), 4)
+        idx = opening * (lax.rem(i, 4) // 2) + (1 - opening) * (i // 4)
+        return kk, idx
+
     def column_at(i):
-        return column(lax.rem(3 * lax.rem(i, 4), 4), i // 4)
+        return column(*source(i))
 
     def copy_wg(c):
         return remote(
             rt.at[0, c],
             rt.at[1, c],
-            rt_send.at[c],
+            rt_send,
             wg_recv.at[c],
             {"dp": mate},
         )
@@ -270,19 +282,19 @@
         return remote(
             nrm_in.at[c],
             nrm_in.at[c],
-            fwd_send.at[kk - 1, idx],
+            fwd_send,
             n_recv.at[c],
             {"mp": peer(kk)},
         )
 
     def copy_cross(c):
         return remote(
-            ssend.at[c], srecv.at[c], s_send.at[c], s_recv.at[c], {"dp": cross}
+            ssend.at[c], srecv.at[c], s_send, s_recv.at[c], {"dp": cross}
         )
 
     def wait_normed(c):
         remote(
-            nrm.at[c], nrm_in.at[c], n_send.at[c], n_recv.at[c], {"dp": mate}
+            nrm.at[c], nrm_in.at[c], n_send, n_recv.at[c], {"dp": mate}
         ).wait_recv()
 
     def forward(idx):
@@ -296,7 +308,7 @@
     def give(i):
         c = column_at(i)
 
-        @pl.when(lax.rem(i, 4) != 0)
+        @pl.when(source(i)[0] != 0)
         def _():
             wait_normed(c)
 
@@ -368,7 +380,7 @@
 
     def copy_sums(kk):
         return remote(
-            sums, sums_in.at[kk], sum_send.at[kk], sum_recv.at[kk], {"mp": peer(kk)}
+            sums, sums_in.at[kk - 1], sum_send, sum_recv.at[kk - 1], {"mp": peer(kk)}
         )
 
     def send_sums():
@@ -384,20 +396,20 @@
     def _():
         lax.fori_loop(2 * chunks, 4 * chunks, part_step, 0)
 
+    @pl.when(jnp.logical_or(outer, sec == 1))
+    def _():
+        send_sums()
+
+    @pl.when(outer)
+    def _():
+        pass_all()
+
     @pl.when(late)
     def _():
         copy_give().start()
         send_normed(0, per_quarter)
         copy_keep(mate_slot).start()
 
-    @pl.when(jnp.logical_or(outer, sec == 1))
-    def _():
-        send_sums()
-
-    @pl.when(outer)
-    def _():
-        pass_all()
-
     @pl.when(early)
     def _():
         send_normed(3, per_quarter)
@@ -408,7 +420,7 @@
         return remote(
             res_ref.at[rows],
             above_in.at[rows],
-            above_send.at[chunk],
+            above_send,
             above_recv.at[chunk],
             {"section": 1 - sec},
         )
@@ -417,7 +429,7 @@
         load_top.wait()
         for kk in (1, 2, 3):
             copy_sums(kk).wait_recv()
-        total = (sums[...] + sums_in[1]) + (sums_in[2] + sums_in[3])
+        total = (sums[...] + sums_in[0]) + (sums_in[1] + sums_in[2])
         total = jnp.concatenate([total] * (LANES // 8), axis=0) * (1.0 / width)
         total = total.T
         acc[0] = jnp.broadcast_to(total[:, 0:1], (tokens, LANES))
@@ -480,19 +492,15 @@
         copy_give().wait_send()
         copy_keep(mate_slot).wait_send()
 
-        def sent(idx, carry):
-            copy_normed(0, idx).wait_send()
-            copy_normed(3, idx).wait_send()
-            return carry
-
-        lax.fori_loop(0, per_quarter, sent, 0)
+        several = pl.ds(0, 2 * per_quarter)
+        sent(nrm.at[several], nrm_in.at[several], n_send)
 
     @pl.when(inner)
     def _():
         def step(i):
             give(i)
             following = i // 4 + 1
-            soon = jnp.logical_and(sec == 0, following == 1)
+            soon = jnp.where(sec == 0, following <= 2, following >= 3)
             turn = lax.rem(i, 4) == jnp.where(soon, 1, 3)
 
             @pl.when(jnp.logical_and(turn, following < per_quarter))
@@ -509,11 +517,11 @@
                 for chunk in range(1, chunks, 2):
                     copy_part(3, chunk).start()
 
-            @pl.when(jnp.logical_and(hold, jnp.logical_and(i >= 6, i < 6 + 2 * chunks)))
-            def _():
-                part_step(i - 6 + 2 * chunks, 0)
-
-            @pl.when(jnp.logical_and(hold, i == 14))
+            @pl.when(jnp.logical_and(hold, jnp.logical_and(i >= 10, i < 10 + 2 * chunks)))
+            def _():
+                part_step(i - 10 + 2 * chunks, 0)
+
+            @pl.when(jnp.logical_and(hold, i == 18))
             def _():
                 send_sums()
 
@@ -527,51 +535,43 @@
                 for chunk in range(1, chunks, 2):
                     copy_part(1 + chunk // upper, chunk).start()
 
-            @pl.when(jnp.logical_and(hold, i == 20))
-            def _():
-                pass_all()
-
             @pl.when(i >= lag)
             def _():
                 theirs(i - lag)
 
-            @pl.when(jnp.logical_and(sec == 1, i == 3))
-            def _():
-                for chunk in range(0, chunks, 2):
-                    copy_part(1 + chunk // upper, chunk).start()
-
-            @pl.when(jnp.logical_and(sec == 1, i == 7))
+            @pl.when(jnp.logical_and(sec == 1, i == 17))
             def _():
                 for chunk in range(1, chunks, 2):
                     copy_part(1 + chunk // upper, chunk).start()
-
-            @pl.when(jnp.logical_and(sec == 1, i == 11))
-            def _():
-                for chunk in range(0, chunks, 2):
-                    pass_on(chunk)
-
-            @pl.when(jnp.logical_and(sec == 1, i == 14))
-            def _():
                 for chunk in range(1, chunks, 2):
                     pass_on(chunk)
 
-            @pl.when(jnp.logical_and(sec == 1, i == 20))
-            def _():
-                residual()
-
-            first_mine = jnp.where(sec == 0, blocks - 4, blocks - 9)
+            first_mine = jnp.where(sec == 0, blocks - 3, blocks - 8)
 
             @pl.when(i == first_mine)
             def _():
                 copy_keep(own_slot).wait_recv()
 
-            @pl.when(jnp.logical_and(i >= first_mine, i < first_mine + 3))
+            @pl.when(jnp.logical_and(sec == 0, i >= blocks - 3))
             def _():
                 for k in range(4):
-                    mine(4 * (i - first_mine) + k)
+                    mine(4 * (i - (blocks - 3)) + k)
+
+            @pl.when(
+                jnp.logical_and(
+                    sec == 1, jnp.logical_and(i >= blocks - 8, i < blocks - 2)
+                )
+            )
+            def _():
+                for k in range(2):
+                    mine(2 * (i - (blocks - 8)) + k)
 
         @pl.when(sec == 1)
         def _():
+            for chunk in range(0, chunks, 2):
+                copy_part(1 + chunk // upper, chunk).start()
+            for chunk in range(0, chunks, 2):
+                pass_on(chunk)
             copy_give().wait_recv()
             forward(0)
 
@@ -581,10 +581,22 @@
 
         lax.fori_loop(1 - sec, blocks, main, 0)
 
+        @pl.when(sec == 0)
+        def _():
+            pass_all()
+
+        @pl.when(sec == 1)
+        def _():
+            residual()
+
         def last_blocks(i, carry):
             theirs(i)
-            for k in range(2):
-                mine(2 * i - blocks + k)
+
+            @pl.when(i >= blocks - 6)
+            def _():
+                for k in range(2):
+                    mine(2 * i - blocks + k)
+
             return carry
 
         lax.fori_loop(blocks - lag, blocks, last_blocks, 0)
@@ -595,36 +607,18 @@
 
         residual_lower()
 
-        def sent(c, carry):
-            copy_cross(c).wait_send()
-            copy_wg(c).wait_send()
-            return carry
-
-        lax.fori_loop(0, blocks, sent, 0)
-
-        def forwarded(idx, carry):
-            copy_forward(1, idx).wait_send()
-            copy_forward(2, idx).wait_send()
-            return carry
-
-        lax.fori_loop(0, per_quarter, forwarded, 0)
-
-    for kk in (1, 2, 3):
-        copy_sums(kk).wait_send()
-
-        def part_sent(chunk, carry):
-            copy_part(kk, chunk).wait_send()
-            return carry
-
-        lax.fori_loop(0, chunks, part_sent, 0)
+        several = pl.ds(0, 2 * per_quarter)
+        sent(ssend, srecv, s_send)
+        sent(nrm_in.at[several], nrm_in.at[several], fwd_send)
+        sent(rt.at[0], rt.at[1], rt_send)
+
+    three = pl.ds(0, 3)
+    sent(sums_in, sums_in, sum_send)
+    sent(psend.at[three], precv.at[three], p_send)
 
     @pl.when(sec == 1)
     def _():
-        def above_sent(chunk, carry):
-            copy_above(chunk).wait_send()
-            return carry
-
-        lax.fori_loop(0, chunks, above_sent, 0)
+        sent(res_ref, above_in, above_send)
 
 
 def fused(value_grad, stream, weights, gain, top_grad, counts):
@@ -677,24 +671,24 @@
             vmem((4, tokens, quarter), BF16),
             vmem((2, tokens, LANES), F32),
             vmem((8, tokens), F32),
-            vmem((4, 8, tokens), F32),
+            vmem((3, 8, tokens), F32),
             vmem((tokens, quarter), BF16),
             vmem((tokens, quarter), F32),
             dma((8,)),
+            dma,
             dma((blocks,)),
-            dma((blocks,)),
-            dma((2, per_quarter)),
+            dma,
             dma((2,)),
             dma((2,)),
+            dma,
             dma((blocks,)),
+            dma,
             dma((blocks,)),
-            dma((blocks,)),
-            dma((blocks,)),
-            dma((4, chunks)),
-            dma((4, chunks)),
-            dma((4,)),
-            dma((4,)),
-            dma((chunks,)),
+            dma,
+            dma((3, chunks)),
+            dma,
+            dma((3,)),
+            dma,
             dma((chunks,)),
         ],
         compiler_params=pltpu.CompilerParams(

time: 77.7 us -> 75.4 us (0.970)
  Pallas kernels: 74.4 us -> 72.1 us
    pallas_call x1, Pallas kernels: 74.4 us -> 72.1 us  [fused(): pl.pallas_call(functools.partial(kernel, (tokens, width, feats, quarter,...]
where the time goes in v5:
time: 75.4 us; the launch traced here: 75.3 us
  Pallas kernels  72.1 us (96%)
  local copies, waits for them, and re-layouts  1.89 us (3%)
  between operations  1.29 us (2%)
    pallas_call x1, Pallas kernels, fused(): pl.pallas_call(functools.partial(kernel, (tokens, width, feats, quarter,...  72.1 us
    unnamed x2, local copies, waits for them, and re-layouts  1.89 us

profile of v5, /device:TPU:1, one launch (start us, length us, event | category | flops | bytes accessed | tf_op | source)
XLA Modules:
  0.0 75.3 jit_solution(7449908547557851380)
XLA Ops:
  1.3 72.1 %shard_map.77 = (bf16[192,3072]{1,0:T(8,128)(2,1)S(1)}, bf16[512,768]{1,0:T(8,128)(2,1)S(1)}) custom-call(bf16[1,512,768]{2,1,0:T(8,128)(2,1)} %vg_hbm.1, bf16[1,512,3072]{2,1,0:T(8,128)(2,1)} %st_hbm.1, bf16[1,768,3072]{2,1,0:T(8,128)(2,1)} %w_hbm.1, f32[1,3072]{1,0:T(1,128)} %gain_hbm.1, bf16[512,3072]{1,0:T(8,128)(2,1)} %top_hbm.1, s32[1]{0:T(128)S(6)} %copy.10.counts_ref), custom_call_target="tpu_custom_call" | custom-call | tf_op jit(solution)/shard_map/pallas_call | solution.py:640
  73.4 1.0 %copy.11 = bf16[1,192,3072]{2,1,0:T(8,128)(2,1)} copy(bf16[1,192,3072]{2,1,0:T(8,128)(2,1)S(1)} %bitcast.2) | data formatting | bytes 2359296
  74.4 0.9 %copy.12 = bf16[1,512,768]{2,1,0:T(8,128)(2,1)} copy(bf16[1,512,768]{2,1,0:T(8,128)(2,1)S(1)} %bitcast.3) | data formatting | bytes 1572864

commit v6 on v5

--- a/solution.py
+++ b/solution.py
@@ -56,8 +56,8 @@
     vgt_recv,
     s_send,
     s_recv,
+    near_recv,
     rt_send,
-    wg_recv,
     p_send,
     p_recv,
     sum_send,
@@ -112,20 +112,20 @@
     load_vg.start()
     load_st = pltpu.make_async_copy(st_hbm.at[0], st_v, load_sem.at[1])
     load_st.start()
-    load_gain = pltpu.make_async_copy(gain_hbm, gain_ref, load_sem.at[7])
+    load_gain = pltpu.make_async_copy(gain_hbm, gain_ref, load_sem.at[4])
     load_gain.start()
 
     def load_w(kk):
         return pltpu.make_async_copy(
             w_hbm.at[0, :, lanes(peer(kk) * quarter, quarter)],
             w_v.at[kk],
-            load_sem.at[2 + kk],
+            load_sem.at[2],
         )
 
     for kk in (3, 2, 1, 0):
         load_w(kk).start()
     load_top = pltpu.make_async_copy(
-        top_hbm.at[:, lanes(m * quarter, quarter)], top_v, load_sem.at[6]
+        top_hbm.at[:, lanes(m * quarter, quarter)], top_v, load_sem.at[3]
     )
     load_top.start()
 
@@ -142,23 +142,26 @@
     @pl.when(inner)
     def _():
         greet({"dp": cross})
-        pl.semaphore_wait(barrier, 6)
-
-    @pl.when(outer)
-    def _():
-        pl.semaphore_wait(barrier, 5)
 
     load_vg.wait()
     half = feats // 2
     for h in range(2):
         vgt[h] = vg_v[:, h * half : (h + 1) * half].T.reshape(2, out_rows, tokens)
 
-    def copy_give():
-        return remote(
-            vgt.at[give_half],
-            vgt_in.at[give_half],
-            vgt_send.at[0],
-            vgt_recv.at[0],
+    @pl.when(inner)
+    def _():
+        pl.semaphore_wait(barrier, 6)
+
+    @pl.when(outer)
+    def _():
+        pl.semaphore_wait(barrier, 5)
+
+    def copy_give(slot, which):
+        return remote(
+            vgt.at[give_half, slot],
+            vgt_in.at[give_half, slot],
+            vgt_send.at[which],
+            vgt_recv.at[which],
             {"dp": mate},
         )
 
@@ -166,8 +169,8 @@
         return remote(
             vgt.at[keep_half, slot],
             vgt_in.at[keep_half, slot],
-            vgt_send.at[1],
-            vgt_recv.at[1],
+            vgt_send.at[2],
+            vgt_recv.at[2],
             {"dp": mate},
         )
 
@@ -176,7 +179,7 @@
 
     @pl.when(early)
     def _():
-        copy_give().start()
+        copy_give(mate_slot, 0).start()
 
     load_gain.wait()
     load_st.wait()
@@ -224,10 +227,13 @@
 
     @pl.when(early)
     def _():
-        send_normed(0, 3)
+        send_normed(0, 1)
+        copy_give(own_slot, 1).start()
+        send_normed(1, 3)
 
     upper = chunks // 2
     lag = 10
+    tail = 8
     hold = jnp.logical_and(inner, sec == 0)
 
     def copy_part(kk, chunk):
@@ -256,24 +262,15 @@
 
         lax.fori_loop(0, chunks, one, 0)
 
-    def source(i):
-        opening = (1 - sec) * (1 - jnp.minimum(i // 8, 1))
-        late_half = lax.rem(i, 8) // 4
-        odd = lax.rem(i, 2)
-        kk = opening * ((1 - late_half) * 3 * odd + late_half * (2 - odd))
-        kk = kk + (1 - opening) * lax.rem(3 * lax.rem(i, 4), 4)
-        idx = opening * (lax.rem(i, 4) // 2) + (1 - opening) * (i // 4)
-        return kk, idx
-
     def column_at(i):
-        return column(*source(i))
+        return column(lax.rem(3 * lax.rem(i, 4), 4), i // 4)
 
     def copy_wg(c):
         return remote(
             rt.at[0, c],
             rt.at[1, c],
             rt_send,
-            wg_recv.at[c],
+            s_recv.at[c],
             {"dp": mate},
         )
 
@@ -292,6 +289,47 @@
             ssend.at[c], srecv.at[c], s_send, s_recv.at[c], {"dp": cross}
         )
 
+    def copy_far(c):
+        return remote(
+            ssend.at[c, own_slot],
+            srecv.at[c, own_slot],
+            s_send,
+            s_recv.at[c],
+            {"dp": cross},
+        )
+
+    def near_slot(i):
+        return lax.rem(i + tail, blocks)
+
+    def copy_near(i):
+        c = column_at(i)
+        return remote(
+            ssend.at[c, mate_slot],
+            srecv.at[c, mate_slot],
+            s_send,
+            near_recv.at[near_slot(i)],
+            {"dp": cross},
+        )
+
+    def wait_far(c):
+        remote(
+            ssend.at[c, mate_slot],
+            srecv.at[c, mate_slot],
+            s_send,
+            s_recv.at[c],
+            {"dp": cross},
+        ).wait_recv()
+
+    def wait_near(i):
+        c = column_at(i)
+        remote(
+            ssend.at[c, own_slot],
+            srecv.at[c, own_slot],
+            s_send,
+            near_recv.at[near_slot(i)],
+            {"dp": cross},
+        ).wait_recv()
+
     def wait_normed(c):
         remote(
             nrm.at[c], nrm_in.at[c], n_send, n_recv.at[c], {"dp": mate}
@@ -308,7 +346,7 @@
     def give(i):
         c = column_at(i)
 
-        @pl.when(source(i)[0] != 0)
+        @pl.when(lax.rem(i, 4) != 0)
         def _():
             wait_normed(c)
 
@@ -316,12 +354,40 @@
         total = dot(vgt[give_half].reshape(rows), nrm[c])
         total = total + dot(vgt_in[give_half].reshape(rows), nrm_in[c])
         ssend[c] = total.astype(BF16).reshape(2, out_rows, LANES)
-        copy_cross(c).start()
-
+
+        @pl.when(i < blocks - tail)
+        def _():
+            copy_cross(c).start()
+
+        @pl.when(i >= blocks - tail)
+        def _():
+            copy_far(c).start()
+
+    def give_rows(i, slot):
+        c = column_at(i)
+        total = dot(vgt[give_half, slot], nrm[c])
+        total = total + dot(vgt_in[give_half, slot], nrm_in[c])
+        ssend[c, slot] = total.astype(BF16)
 
     def theirs(i):
         c = column_at(i)
-        copy_cross(c).wait_recv()
+
+        halves = jnp.logical_or(
+            i >= blocks - tail, jnp.logical_and(sec == 0, i < 2)
+        )
+
+        @pl.when(jnp.logical_not(halves))
+        def _():
+            copy_cross(c).wait_recv()
+
+        @pl.when(halves)
+        def _():
+            wait_far(c)
+
+        @pl.when(jnp.logical_and(sec == 0, i < 2))
+        def _():
+            wait_near(i)
+
         total = dot(vgt[keep_half, mate_slot], nrm[c])
         rt[0, c] = (total + srecv[c, mate_slot].astype(F32)).astype(BF16)
         copy_wg(c).start()
@@ -340,10 +406,6 @@
         chunk = lax.rem(s, chunks)
         rows = row_chunk(chunk)
         q = peer(kk)
-
-        @pl.when(chunk == 0)
-        def _():
-            load_w(kk).wait()
 
         part = jnp.dot(vg_v[rows], w_v[kk], preferred_element_type=F32).astype(BF16)
         psend[kk, rows] = part
@@ -370,17 +432,27 @@
 
         return carry
 
+    pltpu.make_async_copy(w_v, w_v, load_sem.at[2]).wait()
     lax.fori_loop(0, 2 * chunks, part_step, 0)
 
     @pl.when(hold)
     def _():
-        copy_give().wait_recv()
+        copy_give(own_slot, 0).wait_recv()
         forward(0)
-        give(0)
+        give_rows(0, own_slot)
+        copy_far(column_at(0)).start()
+        wait_normed(column_at(1))
+        give_rows(1, own_slot)
+        copy_far(column_at(1)).start()
+        copy_give(mate_slot, 1).wait_recv()
+        for i in range(2):
+            give_rows(i, mate_slot)
+            copy_near(i).start()
+        forward(1)
 
     def copy_sums(kk):
         return remote(
-            sums, sums_in.at[kk - 1], sum_send, sum_recv.at[kk - 1], {"mp": peer(kk)}
+            sums, sums_in.at[kk - 1], sum_send, sum_recv, {"mp": peer(kk)}
         )
 
     def send_sums():
@@ -406,7 +478,8 @@
 
     @pl.when(late)
     def _():
-        copy_give().start()
+        copy_give(mate_slot, 0).start()
+        copy_give(own_slot, 1).start()
         send_normed(0, per_quarter)
         copy_keep(mate_slot).start()
 
@@ -427,8 +500,7 @@
 
     def residual():
         load_top.wait()
-        for kk in (1, 2, 3):
-            copy_sums(kk).wait_recv()
+        remote(sums_in, sums_in, sum_send, sum_recv, {"dp": mate}).wait_recv()
         total = (sums[...] + sums_in[0]) + (sums_in[1] + sums_in[2])
         total = jnp.concatenate([total] * (LANES // 8), axis=0) * (1.0 / width)
         total = total.T
@@ -489,7 +561,8 @@
             return carry
 
         lax.fori_loop(0, blocks, finish, 0)
-        copy_give().wait_send()
+        copy_give(mate_slot, 0).wait_send()
+        copy_give(own_slot, 1).wait_send()
         copy_keep(mate_slot).wait_send()
 
         several = pl.ds(0, 2 * per_quarter)
@@ -500,8 +573,10 @@
         def step(i):
             give(i)
             following = i // 4 + 1
-            soon = jnp.where(sec == 0, following <= 2, following >= 3)
+            soon = jnp.where(sec == 0, following == 2, following >= 3)
             turn = lax.rem(i, 4) == jnp.where(soon, 1, 3)
+
+            turn = jnp.logical_and(turn, jnp.logical_or(sec == 1, following > 1))
 
             @pl.when(jnp.logical_and(turn, following < per_quarter))
             def _():
@@ -543,63 +618,56 @@
             def _():
                 for chunk in range(1, chunks, 2):
                     copy_part(1 + chunk // upper, chunk).start()
-                for chunk in range(1, chunks, 2):
-                    pass_on(chunk)
-
-            first_mine = jnp.where(sec == 0, blocks - 3, blocks - 8)
-
-            @pl.when(i == first_mine)
-            def _():
-                copy_keep(own_slot).wait_recv()
-
-            @pl.when(jnp.logical_and(sec == 0, i >= blocks - 3))
-            def _():
-                for k in range(4):
-                    mine(4 * (i - (blocks - 3)) + k)
-
-            @pl.when(
-                jnp.logical_and(
-                    sec == 1, jnp.logical_and(i >= blocks - 8, i < blocks - 2)
-                )
-            )
-            def _():
-                for k in range(2):
-                    mine(2 * (i - (blocks - 8)) + k)
+                pass_all()
 
         @pl.when(sec == 1)
         def _():
             for chunk in range(0, chunks, 2):
                 copy_part(1 + chunk // upper, chunk).start()
-            for chunk in range(0, chunks, 2):
-                pass_on(chunk)
-            copy_give().wait_recv()
+            copy_give(own_slot, 0).wait_recv()
+            copy_give(mate_slot, 1).wait_recv()
             forward(0)
 
         def main(i, carry):
             step(i)
             return carry
 
-        lax.fori_loop(1 - sec, blocks, main, 0)
+        lax.fori_loop(2 - 2 * sec, blocks, main, 0)
+
+        def send_near(i, carry):
+            copy_near(i).start()
+            return carry
+
+        lax.fori_loop(blocks - tail, blocks, send_near, 0)
 
         @pl.when(sec == 0)
         def _():
             pass_all()
 
+        copy_keep(own_slot).wait_recv()
+
+        def last_far(i, carry):
+            theirs(i)
+
+            @pl.when(i < blocks - 2)
+            def _():
+                for k in range(2):
+                    mine(2 * (i - (blocks - lag)) + k)
+
+            return carry
+
+        lax.fori_loop(blocks - lag, blocks, last_far, 0)
+
         @pl.when(sec == 1)
         def _():
             residual()
 
-        def last_blocks(i, carry):
-            theirs(i)
-
-            @pl.when(i >= blocks - 6)
-            def _():
-                for k in range(2):
-                    mine(2 * i - blocks + k)
-
+        def last_near(i, carry):
+            wait_near(i)
+            mine(i)
             return carry
 
-        lax.fori_loop(blocks - lag, blocks, last_blocks, 0)
+        lax.fori_loop(blocks - tail, blocks, last_near, 0)
 
         @pl.when(sec == 0)
         def _():
@@ -674,20 +742,20 @@
             vmem((3, 8, tokens), F32),
             vmem((tokens, quarter), BF16),
             vmem((tokens, quarter), F32),
-            dma((8,)),
+            dma((5,)),
             dma,
             dma((blocks,)),
             dma,
-            dma((2,)),
-            dma((2,)),
+            dma((3,)),
+            dma((3,)),
             dma,
             dma((blocks,)),
+            dma((10,)),
             dma,
-            dma((blocks,)),
             dma,
             dma((3, chunks)),
             dma,
-            dma((3,)),
+            dma,
             dma,
             dma((chunks,)),
         ],
@@ -695,7 +763,31 @@
             collective_id=0, has_side_effects=True, vmem_limit_bytes=51 * 2**20
         ),
     )(*placed, counts)
+    held = [
+        pltpu.with_memory_space_constraint(a, pltpu.VMEM)
+        for a in (weight_grad, residual_grad)
+    ]
+    weight_grad, residual_grad = pl.pallas_call(
+        store,
+        out_shape=tuple(jax.ShapeDtypeStruct(a.shape, a.dtype) for a in held),
+        in_specs=[in_vmem, in_vmem],
+        out_specs=(in_hbm, in_hbm),
+        scratch_shapes=[dma((4,))],
+    )(*held)
     return weight_grad[None], residual_grad[None]
+
+
+def store(weight_ref, residual_ref, weight_out, residual_out, sem):
+    copies = []
+    for k, (src, dst) in enumerate(((weight_ref, weight_out), (residual_ref, residual_out))):
+        half = src.shape[0] // 2
+        for h in range(2):
+            rows = pl.ds(h * half, half)
+            copies.append(pltpu.make_async_copy(src.at[rows], dst.at[rows], sem.at[2 * k + h]))
+    for copy in copies:
+        copy.start()
+    for copy in copies:
+        copy.wait()
 
 
 def normalize(stream_rows):

time: 75.4 us -> 70.5 us (0.935)
  Pallas kernels: 72.1 us -> 69 us
  local copies, waits for them, and re-layouts: 1.89 us -> 0 us
    pallas_call x1, Pallas kernels: 72.1 us -> 67.7 us  [fused(): pl.pallas_call(functools.partial(kernel, (tokens, width, feats, quarter,...]
    unnamed x2 -> x0, local copies, waits for them, and re-layouts: 1.89 us -> none
    pallas_call x0 -> x1, Pallas kernels: none -> 1.3 us  [fused(): pl.pallas_call(store, out_shape=tuple((jax.ShapeDtypeStruct(a.shape, a.dt...]
where the time goes in v6:
time: 70.5 us; the launch traced here: 70.3 us
  Pallas kernels  69 us (98%)
  between operations  1.29 us (2%)
    pallas_call x1, Pallas kernels, fused(): pl.pallas_call(functools.partial(kernel, (tokens, width, feats, quarter,...  67.7 us

profile of v6, /device:TPU:1, one launch (start us, length us, event | category | flops | bytes accessed | tf_op | source)
XLA Modules:
  0.0 70.3 jit_solution(16219374139216912245)
XLA Ops:
  1.3 67.7 %shard_map.77 = (bf16[192,3072]{1,0:T(8,128)(2,1)S(1)}, bf16[512,768]{1,0:T(8,128)(2,1)S(1)}) custom-call(bf16[1,512,768]{2,1,0:T(8,128)(2,1)} %vg_hbm.1, bf16[1,512,3072]{2,1,0:T(8,128)(2,1)} %st_hbm.1, bf16[1,768,3072]{2,1,0:T(8,128)(2,1)} %w_hbm.1, f32[1,3072]{1,0:T(1,128)} %gain_hbm.1, bf16[512,3072]{1,0:T(8,128)(2,1)} %top_hbm.1, s32[1]{0:T(128)S(6)} %copy.8.counts_ref), custom_call_target="tpu_custom_call" | custom-call | tf_op jit(solution)/shard_map/pallas_call | solution.py:708
  69.0 1.3 %shard_map.78 = (bf16[192,3072]{1,0:T(8,128)(2,1)}, bf16[512,768]{1,0:T(8,128)(2,1)}) custom-call(bf16[192,3072]{1,0:T(8,128)(2,1)S(1)} %get-tuple-element.6.weight_ref, bf16[512,768]{1,0:T(8,128)(2,1)S(1)} %get-tuple-element.7.residual_ref), custom_call_target="tpu_custom_call" | custom-call | tf_op jit(solution)/shard_map/pallas_call | solution.py:770

commit v7 on v6

--- a/solution.py
+++ b/solution.py
@@ -10,7 +10,7 @@
 TOK_MB = 256
 LANES = 128
 ROWS = 128
-LN_ROWS = 64
+LN_ROWS = 128
 EPS = 1e-06
 F32 = jnp.float32
 BF16 = jnp.bfloat16
@@ -41,6 +41,7 @@
     ssend,
     srecv,
     rt,
+    kept,
     psend,
     precv,
     acc,
@@ -134,7 +135,7 @@
     def greet(where):
         pl.semaphore_signal(barrier, inc=1, device_id=where, device_id_type=MESH)
 
-    for kk in (1, 2, 3):
+    for kk in (1, 2):
         greet({"mp": peer(kk)})
     greet({"dp": mate})
     greet({"section": 1 - sec})
@@ -150,11 +151,11 @@
 
     @pl.when(inner)
     def _():
-        pl.semaphore_wait(barrier, 6)
+        pl.semaphore_wait(barrier, 5)
 
     @pl.when(outer)
     def _():
-        pl.semaphore_wait(barrier, 5)
+        pl.semaphore_wait(barrier, 4)
 
     def copy_give(slot, which):
         return remote(
@@ -255,6 +256,20 @@
         psend[kk, rows] = (psend[kk, rows].astype(F32) + precv[3, rows].astype(F32)).astype(BF16)
         copy_part(kk, chunk).start()
 
+    def copy_sums(step):
+        return remote(
+            sums.at[step],
+            sums_in.at[step],
+            sum_send.at[step],
+            sum_recv.at[step],
+            {"mp": peer(step + 1)},
+        )
+
+    def pass_sums():
+        copy_sums(0).wait_recv()
+        sums[1] = sums[0] + sums_in[0]
+        copy_sums(1).start()
+
     def pass_all():
         def one(chunk, carry):
             pass_on(chunk)
@@ -371,7 +386,8 @@
 
     def theirs(i):
         c = column_at(i)
-
+        total = dot(vgt[keep_half].reshape(2 * out_rows, tokens), nrm[c])
+        kept[c] = total.reshape(2, out_rows, LANES)
         halves = jnp.logical_or(
             i >= blocks - tail, jnp.logical_and(sec == 0, i < 2)
         )
@@ -388,14 +404,15 @@
         def _():
             wait_near(i)
 
-        total = dot(vgt[keep_half, mate_slot], nrm[c])
-        rt[0, c] = (total + srecv[c, mate_slot].astype(F32)).astype(BF16)
+        total = kept[c, mate_slot] + srecv[c, mate_slot].astype(F32)
+        rt[0, c] = total.astype(BF16)
         copy_wg(c).start()
 
-    def mine(i):
+    def mine(i, near=False):
         c = column_at(i)
-        total = dot(vgt[keep_half, own_slot], nrm[c])
-        total = total + dot(vgt_in[keep_half, own_slot], nrm_in[c])
+        total = kept[c, own_slot] + dot(vgt_in[keep_half, own_slot], nrm_in[c])
+        if near:
+            wait_near(i)
         total = total + srecv[c, own_slot].astype(F32)
         wg_ref[:, lanes(c * LANES)] = total.astype(BF16)
 
@@ -448,21 +465,14 @@
         for i in range(2):
             give_rows(i, mate_slot)
             copy_near(i).start()
-        forward(1)
-
-    def copy_sums(kk):
-        return remote(
-            sums, sums_in.at[kk - 1], sum_send, sum_recv, {"mp": peer(kk)}
-        )
 
     def send_sums():
         lane = lax.broadcasted_iota(jnp.int32, (tokens, LANES), 1)
         sum0 = jnp.sum(acc[0], axis=-1, keepdims=True)
         sum1 = jnp.sum(acc[1], axis=-1, keepdims=True)
         packed = jnp.where(lane == 0, sum0, jnp.where(lane == 1, sum1, 0.0))
-        sums[...] = packed.T[:8]
-        for kk in (3, 2, 1):
-            copy_sums(kk).start()
+        sums[0] = packed.T[:8]
+        copy_sums(0).start()
 
     @pl.when(jnp.logical_or(outer, sec == 1))
     def _():
@@ -500,8 +510,8 @@
 
     def residual():
         load_top.wait()
-        remote(sums_in, sums_in, sum_send, sum_recv, {"dp": mate}).wait_recv()
-        total = (sums[...] + sums_in[0]) + (sums_in[1] + sums_in[2])
+        copy_sums(1).wait_recv()
+        total = sums[1] + sums_in[1]
         total = jnp.concatenate([total] * (LANES // 8), axis=0) * (1.0 / width)
         total = total.T
         acc[0] = jnp.broadcast_to(total[:, 0:1], (tokens, LANES))
@@ -550,6 +560,7 @@
 
     @pl.when(outer)
     def _():
+        pass_sums()
         residual()
         residual_lower()
 
@@ -574,9 +585,8 @@
             give(i)
             following = i // 4 + 1
             soon = jnp.where(sec == 0, following == 2, following >= 3)
-            turn = lax.rem(i, 4) == jnp.where(soon, 1, 3)
-
-            turn = jnp.logical_and(turn, jnp.logical_or(sec == 1, following > 1))
+            usual = jnp.where(jnp.logical_and(sec == 0, following == 1), 2, 3)
+            turn = lax.rem(i, 4) == jnp.where(soon, 1, usual)
 
             @pl.when(jnp.logical_and(turn, following < per_quarter))
             def _():
@@ -616,14 +626,13 @@
 
             @pl.when(jnp.logical_and(sec == 1, i == 17))
             def _():
-                for chunk in range(1, chunks, 2):
+                for chunk in range(chunks):
                     copy_part(1 + chunk // upper, chunk).start()
+                pass_sums()
                 pass_all()
 
         @pl.when(sec == 1)
         def _():
-            for chunk in range(0, chunks, 2):
-                copy_part(1 + chunk // upper, chunk).start()
             copy_give(own_slot, 0).wait_recv()
             copy_give(mate_slot, 1).wait_recv()
             forward(0)
@@ -642,6 +651,7 @@
 
         @pl.when(sec == 0)
         def _():
+            pass_sums()
             pass_all()
 
         copy_keep(own_slot).wait_recv()
@@ -663,8 +673,7 @@
             residual()
 
         def last_near(i, carry):
-            wait_near(i)
-            mine(i)
+            mine(i, near=True)
             return carry
 
         lax.fori_loop(blocks - tail, blocks, last_near, 0)
@@ -681,7 +690,8 @@
         sent(rt.at[0], rt.at[1], rt_send)
 
     three = pl.ds(0, 3)
-    sent(sums_in, sums_in, sum_send)
+    for step in range(2):
+        copy_sums(step).wait_send()
     sent(psend.at[three], precv.at[three], p_send)
 
     @pl.when(sec == 1)
@@ -735,11 +745,12 @@
             vmem((blocks, 2, out_rows, LANES), BF16),
             vmem((blocks, 2, out_rows, LANES), BF16),
             vmem((2, blocks, out_rows, LANES), BF16),
+            vmem((blocks, 2, out_rows, LANES), F32),
             vmem((4, tokens, quarter), BF16),
             vmem((4, tokens, quarter), BF16),
             vmem((2, tokens, LANES), F32),
-            vmem((8, tokens), F32),
-            vmem((3, 8, tokens), F32),
+            vmem((2, 8, tokens), F32),
+            vmem((2, 8, tokens), F32),
             vmem((tokens, quarter), BF16),
             vmem((tokens, quarter), F32),
             dma((5,)),
@@ -754,8 +765,8 @@
             dma,
             dma,
             dma((3, chunks)),
-            dma,
-            dma,
+            dma((2,)),
+            dma((2,)),
             dma,
             dma((chunks,)),
         ],

time: 70.5 us -> 69.7 us (0.989)
  Pallas kernels: 69 us -> 68.1 us
    pallas_call x1, Pallas kernels: 67.7 us -> 66.8 us  [fused(): pl.pallas_call(functools.partial(kernel, (tokens, width, feats, quarter,...]
where the time goes in v7:
time: 69.7 us; the launch traced here: 69.4 us
  Pallas kernels  68.1 us (98%)
  between operations  1.29 us (2%)
    pallas_call x1, Pallas kernels, fused(): pl.pallas_call(functools.partial(kernel, (tokens, width, feats, quarter,...  66.8 us

profile of v7, /device:TPU:1, one launch (start us, length us, event | category | flops | bytes accessed | tf_op | source)
XLA Modules:
  0.0 69.4 jit_solution(14649568093610308822)
XLA Ops:
  1.3 66.8 %shard_map.77 = (bf16[192,3072]{1,0:T(8,128)(2,1)S(1)}, bf16[512,768]{1,0:T(8,128)(2,1)S(1)}) custom-call(bf16[1,512,768]{2,1,0:T(8,128)(2,1)} %vg_hbm.1, bf16[1,512,3072]{2,1,0:T(8,128)(2,1)} %st_hbm.1, bf16[1,768,3072]{2,1,0:T(8,128)(2,1)} %w_hbm.1, f32[1,3072]{1,0:T(1,128)} %gain_hbm.1, bf16[512,3072]{1,0:T(8,128)(2,1)} %top_hbm.1, s32[1]{0:T(128)S(6)} %copy.8.counts_ref), custom_call_target="tpu_custom_call" | custom-call | tf_op jit(solution)/shard_map/pallas_call | solution.py:718
  68.1 1.3 %shard_map.78 = (bf16[192,3072]{1,0:T(8,128)(2,1)}, bf16[512,768]{1,0:T(8,128)(2,1)}) custom-call(bf16[192,3072]{1,0:T(8,128)(2,1)S(1)} %get-tuple-element.6.weight_ref, bf16[512,768]{1,0:T(8,128)(2,1)S(1)} %get-tuple-element.7.residual_ref), custom_call_target="tpu_custom_call" | custom-call | tf_op jit(solution)/shard_map/pallas_call | solution.py:781

commit v8 on v7

--- a/solution.py
+++ b/solution.py
@@ -783,7 +783,7 @@
         out_shape=tuple(jax.ShapeDtypeStruct(a.shape, a.dtype) for a in held),
         in_specs=[in_vmem, in_vmem],
         out_specs=(in_hbm, in_hbm),
-        scratch_shapes=[dma((4,))],
+        scratch_shapes=[dma((8,))],
     )(*held)
     return weight_grad[None], residual_grad[None]
 
@@ -791,10 +791,10 @@
 def store(weight_ref, residual_ref, weight_out, residual_out, sem):
     copies = []
     for k, (src, dst) in enumerate(((weight_ref, weight_out), (residual_ref, residual_out))):
-        half = src.shape[0] // 2
-        for h in range(2):
-            rows = pl.ds(h * half, half)
-            copies.append(pltpu.make_async_copy(src.at[rows], dst.at[rows], sem.at[2 * k + h]))
+        share = src.shape[0] // 4
+        for h in range(4):
+            rows = pl.ds(h * share, share)
+            copies.append(pltpu.make_async_copy(src.at[rows], dst.at[rows], sem.at[4 * k + h]))
     for copy in copies:
         copy.start()
     for copy in copies:

time: 69.7 us -> 69.8 us (level)
  no operation moved by 1% of the time
where the time goes in v8:
time: 69.8 us; the launch traced here: 69.5 us
  Pallas kernels  68.2 us (98%)
  between operations  1.29 us (2%)
    pallas_call x1, Pallas kernels, fused(): pl.pallas_call(functools.partial(kernel, (tokens, width, feats, quarter,...  66.8 us

profile of v8, /device:TPU:1, one launch (start us, length us, event | category | flops | bytes accessed | tf_op | source)
XLA Modules:
  0.0 69.5 jit_solution(14803911332598646079)
XLA Ops:
  1.3 66.8 %shard_map.77 = (bf16[192,3072]{1,0:T(8,128)(2,1)S(1)}, bf16[512,768]{1,0:T(8,128)(2,1)S(1)}) custom-call(bf16[1,512,768]{2,1,0:T(8,128)(2,1)} %vg_hbm.1, bf16[1,512,3072]{2,1,0:T(8,128)(2,1)} %st_hbm.1, bf16[1,768,3072]{2,1,0:T(8,128)(2,1)} %w_hbm.1, f32[1,3072]{1,0:T(1,128)} %gain_hbm.1, bf16[512,3072]{1,0:T(8,128)(2,1)} %top_hbm.1, s32[1]{0:T(128)S(6)} %copy.8.counts_ref), custom_call_target="tpu_custom_call" | custom-call | tf_op jit(solution)/shard_map/pallas_call | solution.py:718
  68.1 1.3 %shard_map.78 = (bf16[192,3072]{1,0:T(8,128)(2,1)}, bf16[512,768]{1,0:T(8,128)(2,1)}) custom-call(bf16[192,3072]{1,0:T(8,128)(2,1)S(1)} %get-tuple-element.6.weight_ref, bf16[512,768]{1,0:T(8,128)(2,1)S(1)} %get-tuple-element.7.residual_ref), custom_call_target="tpu_custom_call" | custom-call | tf_op jit(solution)/shard_map/pallas_call | solution.py:781
